TPU v7x, 32 devices: a 4x4x1 block of a 4x4x8 slice. The times are simulated.
32 devices in a mesh: pair: 1 (over z), tp: 4 (over y), side: 8 (over x, core).
Axes of the slice: x: 4, y: 4, z: 1, core: 2. Of those that a mesh axis runs over, the one named last changes fastest.
The devices are a block of a 4x4x8 slice.
Arguments:
- prompt_x: bfloat16 [1024, 4096], P(('pair', 'side'))
- s_len: int32 [8], P(('pair', 'side'))
- w_qkv_pre: bfloat16 [1, 4096, 3, 32, 128], P(None, None, None, 'tp')
- w_out_pre: bfloat16 [1, 32, 128, 4096], P(None, 'tp')
- w_gu_pre: bfloat16 [1, 2, 11008, 4096], P(None, None, 'tp')
- w_down_pre: bfloat16 [1, 11008, 4096], P(None, 'tp')
- gain_pre: float32 [1, 2, 4096], replicated
- dec_tokens: bfloat16 [64, 4096], P(('pair', 'side'))
- k_cache: bfloat16 [1, 64, 256, 8, 4, 128], P(None, ('pair', 'side'), None, None, 'tp')
- v_cache: bfloat16 [1, 64, 256, 8, 4, 128], P(None, ('pair', 'side'), None, None, 'tp')
- c_len: int32 [64], P(('pair', 'side'))
- w_qkv_dec: bfloat16 [1, 4096, 3, 8, 4, 128], P(None, None, None, None, 'tp')
- w_out_dec: bfloat16 [1, 8, 4, 128, 4096], P(None, None, 'tp')
- w_gu_dec: bfloat16 [1, 2, 11008, 4096], P(None, None, 'tp')
- w_down_dec: bfloat16 [1, 11008, 4096], P(None, 'tp')
- gain_dec: float32 [1, 2, 4096], replicated
Outputs:
- output 1: bfloat16 [1024, 4096], P(('pair', 'side'))
- output 2: bfloat16 [64, 4096], P(('pair', 'side'))
- output 3: bfloat16 [1, 1024, 8, 4, 128], P(None, ('pair', 'side'), None, 'tp')
- output 4: bfloat16 [1, 1024, 8, 4, 128], P(None, ('pair', 'side'), None, 'tp')
- output 5: bfloat16 [1, 64, 256, 8, 4, 128], P(None, ('pair', 'side'), None, None, 'tp')
- output 6: bfloat16 [1, 64, 256, 8, 4, 128], P(None, ('pair', 'side'), None, None, 'tp')
All inputs are finite; a program needn't handle non-finite values.
Results may differ from a plain program's by a relative error of at most 0.0125934.
Values are sent between devices in bfloat16 or wider.
A program may use at most 768 MiB of HBM per device.

v0:
```python
import jax
import jax.numpy as jnp
from jax import lax
from jax.sharding import PartitionSpec as P

EPSILON = 1e-6
THETA = 10000.0
MASKED = -1e30


def rms_norm(hidden, gain_vec):
    hid_f32 = hidden.astype(jnp.float32)
    inv_rms = lax.rsqrt(jnp.mean(hid_f32 * hid_f32, axis=-1, keepdims=True) + EPSILON)
    return (hid_f32 * inv_rms * gain_vec).astype(jnp.bfloat16)


def add_residual(hidden, update):
    return (hidden.astype(jnp.float32) + update.astype(jnp.float32)).astype(jnp.bfloat16)


def rope_tables(positions, head_dim):
    half_dim = head_dim // 2
    inv_freq = THETA ** (-jnp.arange(half_dim, dtype=jnp.float32) * 2.0 / head_dim)
    angles = positions.astype(jnp.float32)[:, None] * inv_freq[None, :]
    return jnp.cos(angles), jnp.sin(angles)


def apply_rope(values_in, cos_tab, sin_tab):
    half_dim = values_in.shape[-1] // 2
    lower_half = values_in[..., :half_dim]
    upper_half = values_in[..., half_dim:]
    cos_b = cos_tab[:, None, :]
    sin_b = sin_tab[:, None, :]
    return jnp.concatenate([lower_half * cos_b - upper_half * sin_b, upper_half * cos_b + lower_half * sin_b], axis=-1)


def swiglu(hidden, gain_vec, w_gu, w_down):
    normed = rms_norm(hidden, gain_vec)
    gate_up = jnp.einsum('...d,kfd->...kf', normed, w_gu, preferred_element_type=jnp.float32)
    gate_val = gate_up[..., 0, :].astype(jnp.bfloat16).astype(jnp.float32)
    up_val = gate_up[..., 1, :].astype(jnp.bfloat16).astype(jnp.float32)
    activated = (jax.nn.silu(gate_val) * up_val).astype(jnp.bfloat16)
    return jnp.einsum('...f,fd->...d', activated, w_down, preferred_element_type=jnp.float32)


def prompt_attention(queries, keys_in, values_in, allowed):
    attn_scale = queries.shape[-1] ** -0.5
    scores = jnp.einsum('nqhe,nkhe->nhqk', queries, keys_in, preferred_element_type=jnp.float32) * attn_scale
    scores = jnp.where(allowed[:, None], scores, MASKED)
    prob_bf = jax.nn.softmax(scores, axis=-1).astype(jnp.bfloat16)
    return jnp.einsum('nhqk,nkhe->nqhe', prob_bf, values_in, preferred_element_type=jnp.float32).astype(jnp.bfloat16)


def decode_attention(queries, k_tok, v_tok, k_layer, v_layer, visible):
    attn_scale = queries.shape[-1] ** -0.5
    cache_scores = jnp.einsum('bhe,bthe->bht', queries, k_layer, preferred_element_type=jnp.float32) * attn_scale
    cache_scores = jnp.where(visible, cache_scores, MASKED)
    self_score = jnp.einsum('bhe,bhe->bh', queries, k_tok, preferred_element_type=jnp.float32) * attn_scale
    row_max = jnp.maximum(jnp.max(cache_scores, axis=-1), self_score)
    cache_exp = jnp.exp(cache_scores - row_max[..., None])
    self_exp = jnp.exp(self_score - row_max)
    denominator = jnp.sum(cache_exp, axis=-1) + self_exp
    cache_prob = (cache_exp / denominator[..., None]).astype(jnp.bfloat16)
    self_prob = (self_exp / denominator).astype(jnp.bfloat16).astype(jnp.float32)
    context = jnp.einsum('bht,bthe->bhe', cache_prob, v_layer, preferred_element_type=jnp.float32) + self_prob[..., None] * v_tok.astype(jnp.float32)
    return context.astype(jnp.bfloat16)


def run_prefill(prompts, s_valid, w_qkv, w_out, w_gu, w_down, gains):
    seq_len = prompts.shape[1]
    positions = jnp.arange(seq_len)
    cos_tab, sin_tab = rope_tables(positions, w_qkv.shape[-1])
    allowed = (positions[None, :] <= positions[:, None])[None] & (positions[None, None, :] < s_valid[:, None, None])
    hidden = prompts
    kv_layers = []
    for layer_idx in range(w_qkv.shape[0]):
        normed = rms_norm(hidden, gains[layer_idx, 0])
        qkv_out = jnp.einsum('nsd,dkhe->nskhe', normed, w_qkv[layer_idx], preferred_element_type=jnp.float32)
        queries = apply_rope(qkv_out[:, :, 0], cos_tab, sin_tab).astype(jnp.bfloat16)
        keys_new = apply_rope(qkv_out[:, :, 1], cos_tab, sin_tab).astype(jnp.bfloat16)
        values_new = qkv_out[:, :, 2].astype(jnp.bfloat16)
        context = prompt_attention(queries, keys_new, values_new, allowed)
        part_sum = jnp.einsum('nshe,hed->nsd', context, w_out[layer_idx], preferred_element_type=jnp.float32)
        hidden = add_residual(hidden, lax.psum(part_sum, 'tp').astype(jnp.bfloat16))
        mlp_part = swiglu(hidden, gains[layer_idx, 1], w_gu[layer_idx], w_down[layer_idx])
        hidden = add_residual(hidden, lax.psum(mlp_part, 'tp').astype(jnp.bfloat16))
        kv_layers.append(jnp.stack([keys_new, values_new]))
    return hidden, kv_layers


def run_decode(tokens, k_cache, v_cache, c_len, w_qkv, w_out, w_gu, w_down, gains):
    layers = k_cache.shape[0]
    row_count = k_cache.shape[1]
    cache_len = k_cache.shape[2]
    heads_loc = k_cache.shape[3]
    head_dim = k_cache.shape[5]
    model_width = tokens.shape[1]
    k_local = k_cache.reshape(layers, row_count, cache_len, heads_loc, head_dim)
    v_local = v_cache.reshape(layers, row_count, cache_len, heads_loc, head_dim)
    wqkv_local = w_qkv.reshape(layers, model_width, 3, heads_loc, head_dim)
    wout_local = w_out.reshape(layers, heads_loc, head_dim, model_width)
    cos_tab, sin_tab = rope_tables(c_len, head_dim)
    cache_pos = jnp.arange(cache_len)
    visible = (cache_pos[None, :] < c_len[:, None])[:, None, :]
    write_at = (cache_pos[None, :] == c_len[:, None])[:, :, None, None]
    k_next = []
    v_next = []
    for layer_idx in range(layers):
        normed = rms_norm(tokens, gains[layer_idx, 0])
        qkv_out = jnp.einsum('bd,dkhe->bkhe', normed, wqkv_local[layer_idx], preferred_element_type=jnp.float32)
        queries = apply_rope(qkv_out[:, 0], cos_tab, sin_tab).astype(jnp.bfloat16)
        k_tok = apply_rope(qkv_out[:, 1], cos_tab, sin_tab).astype(jnp.bfloat16)
        v_tok = qkv_out[:, 2].astype(jnp.bfloat16)
        context = decode_attention(queries, k_tok, v_tok, k_local[layer_idx], v_local[layer_idx], visible)
        part_sum = jnp.einsum('bhe,hed->bd', context, wout_local[layer_idx], preferred_element_type=jnp.float32)
        tokens = add_residual(tokens, lax.psum(part_sum, 'tp').astype(jnp.bfloat16))
        mlp_part = swiglu(tokens, gains[layer_idx, 1], w_gu[layer_idx], w_down[layer_idx])
        tokens = add_residual(tokens, lax.psum(mlp_part, 'tp').astype(jnp.bfloat16))
        k_next.append(jnp.where(write_at, k_tok[:, None], k_local[layer_idx]))
        v_next.append(jnp.where(write_at, v_tok[:, None], v_local[layer_idx]))
    return tokens, jnp.stack(k_next).reshape(k_cache.shape), jnp.stack(v_next).reshape(v_cache.shape)


def heads_to_rows(kv_local, tp_size):
    pair_kv, seq_len, heads_loc, head_dim = kv_local.shape
    by_block = kv_local.reshape(pair_kv, tp_size, seq_len // tp_size, heads_loc, head_dim)
    gathered = lax.all_to_all(by_block, 'tp', 1, 2)
    return gathered.reshape(pair_kv, seq_len // tp_size, tp_size * heads_loc, head_dim)


def rows_to_heads(kv_rows, tp_size):
    pair_kv, seq_part, heads_all, head_dim = kv_rows.shape
    grouped = kv_rows.reshape(pair_kv, seq_part, heads_all // tp_size, tp_size, head_dim)
    spread = lax.all_to_all(grouped, 'tp', 3, 1)
    return spread.reshape(pair_kv, tp_size * seq_part, heads_all // tp_size, head_dim)


def solution(mesh):
    tp_size = mesh.shape['tp']
    side_size = mesh.shape['side']
    partner_perm = [(src_idx, (src_idx + side_size // 2) % side_size) for src_idx in range(side_size)]
    inst_axes = ('pair', 'side')
    rows_spec = P(inst_axes, None)
    vec_spec = P(inst_axes)
    cache_spec = P(None, inst_axes, None, None, 'tp', None)
    prompt_spec = P(None, inst_axes, None, 'tp', None)
    in_specs = (rows_spec, vec_spec, P(None, None, None, 'tp', None), P(None, 'tp', None, None), P(None, None, 'tp', None), P(None, 'tp', None), P(None, None, None), rows_spec, cache_spec, cache_spec, vec_spec, P(None, None, None, None, 'tp', None), P(None, None, 'tp', None, None), P(None, None, 'tp', None), P(None, 'tp', None), P(None, None, None))
    out_specs = (rows_spec, rows_spec, prompt_spec, prompt_spec, cache_spec, cache_spec)

    def device_fn(prompt_x, s_len, w_qkv_pre, w_out_pre, w_gu_pre, w_down_pre, gain_pre, dec_tokens, k_cache, v_cache, c_len, w_qkv_dec, w_out_dec, w_gu_dec, w_down_dec, gain_dec):
        hidden, kv_layers = run_prefill(prompt_x[None], s_len, w_qkv_pre, w_out_pre, w_gu_pre, w_down_pre, gain_pre)
        installed = []
        for kv_layer in kv_layers:
            kv_rows = heads_to_rows(kv_layer[:, 0], tp_size)
            kv_rows = lax.ppermute(kv_rows, 'side', partner_perm)
            installed.append(rows_to_heads(kv_rows, tp_size))
        prompt_kv = jnp.stack(installed, axis=1)[:, :, :, :, None, :]
        dec_out, k_cache_new, v_cache_new = run_decode(dec_tokens, k_cache, v_cache, c_len, w_qkv_dec, w_out_dec, w_gu_dec, w_down_dec, gain_dec)
        return hidden[0], dec_out, prompt_kv[0], prompt_kv[1], k_cache_new, v_cache_new

    return jax.shard_map(device_fn, mesh=mesh, in_specs=in_specs, out_specs=out_specs, check_vma=False)
```

profile of v0, /device:TPU:100, one launch (start us, length us, event | category | flops | bytes accessed | tf_op | source)
XLA Modules:
  0.0 261.6 jit_solution(13822593241111800580)
XLA Ops:
  0.7 31.4 %copy.86 = bf16[4096,3,8,128]{0,3,2,1:T(8,128)(2,1)} copy(bf16[4096,3,8,128]{3,2,1,0:T(8,128)(2,1)} %bitcast.156) | data formatting | bytes 50331648 | tf_op jit(solution)/shard_map/squeeze | solution.py:78
  32.5 11.8 %fusion.58 = f32[128,3072]{0,1:S(1)} fusion(bf16[4096,3072]{0,1:T(8,128)(2,1)} %bitcast.155, bf16[128,4096]{1,0:T(8,128)(2,1)S(1)} %copy-done, f32[4096]{0:T(1024)S(1)} %bitcast.174, f32[128]{0:T(128)S(1)} %add_rsqrt_fusion.3), kind=kOutput, calls=%fused_computation.57 | convolution fusion | flops 3223322624 | bytes 27804160
  44.3 1.0 copy-done.1
  46.5 0.8 copy.96
  47.4 5.9 %all-to-all-start = ((bf16[2,4,32,1,8,128]{5,4,2,3,0,1:T(8,128)(2,1)}), bf16[2,4,32,1,8,128]{5,4,2,3,0,1:T(8,128)(2,1)}, u32[]{:S(2)}, u32[]{:S(2)}) async-start(bf16[2,4,32,1,8,128]{5,4,2,3,0,1:T(8,128)(2,1)} %copy.96), calls=%async_computation | async-start | bytes 1048576 | tf_op jit(solution)/shard_map/all_to_all | solution.py:127
  54.5 6.4 %fusion.15 = f32[1,128,4096]{2,1,0:T(8,128)} fusion(bf16[1,8,128,4096]{3,2,1,0:T(8,128)(2,1)} %param.19, f32[8,128,128]{1,2,0:T(8,128)S(1)} %get-tuple-element.67, f32[8,128]{1,0:T(8,128)S(1)} %get-tuple-element.66, f32[1,128,3,8,128]{1,4,3,2,0:T(8,128)} %bitcast.161), kind=kOutput, calls=%fused_computation.15 | convolution fusion | flops 1107689472 | bytes 11276288 | tf_op jit(solution)/shard_map/nshe,hed->nsd/dot_general | solution.py:83
  61.1 11.5 %fusion.5 = f32[8,3,8,128]{3,0,2,1:T(8,128)S(1)} fusion(bf16[4096,3,8,128]{3,2,1,0:T(8,128)(2,1)} %bitcast.157, bf16[8,4096]{1,0:T(8,128)(2,1)S(1)} %copy-done.2, f32[4096]{0:T(1024)S(1)} %bitcast.176, f32[8]{0:T(128)S(1)} %add_rsqrt_fusion.1), kind=kOutput, calls=%fused_computation.5 | convolution fusion | flops 201457664 | bytes 25346080 | tf_op jit(solution)/shard_map/bd,dkhe->bkhe/dot_general | solution.py:110
  73.1 3.4 %fusion.26 = f32[8,8,1,256]{3,2,1,0:T(1,128)S(1)} fusion(bf16[8,256,8,128]{3,2,1,0:T(8,128)(2,1)} %bitcast.158, bf16[8,8,128,1]{2,0,1,3:T(8,128)(2,1)S(1)} %fusion.117), kind=kOutput, calls=%fused_computation.20 | convolution fusion | flops 4194304 | bytes 4276224 | tf_op jit(solution)/shard_map/bhe,bthe->bht/dot_general | solution.py:56
  77.0 2.8 %fusion.24 = f32[8,8,1,128]{3,2,1,0:T(1,128)S(1)} fusion(bf16[8,256,8,128]{3,2,1,0:T(8,128)(2,1)} %bitcast.162, bf16[8,8,256,1]{2,1,0,3:T(8,128)(2,1)S(1)} %fusion.113), kind=kOutput, calls=%fused_computation.18 | convolution fusion | flops 4194304 | bytes 4259840 | tf_op jit(solution)/shard_map/bht,bthe->bhe/dot_general | solution.py:65
  79.8 4.6 %fusion.21 = f32[8,4096]{1,0:T(8,128)S(1)} fusion(bf16[1,8,1,128,4096]{4,3,2,1,0:T(8,128)(2,1)} %param.28, f32[8,8,1,128]{3,2,1,0:T(1,128)S(1)} %fusion.24, f32[8,8]{0,1:T(8,128)S(1)} %copy.92, f32[8,3,8,128]{3,0,2,1:T(8,128)S(1)} %fusion.5), kind=kOutput, calls=%fused_computation.17 | convolution fusion | flops 67141632 | bytes 8572928 | tf_op jit(solution)/shard_map/bhe,hed->bd/dot_general | solution.py:115
  84.5 46.1 %all-reduce.4 = (bf16[1,128,4096]{2,1,0:T(8,128)(2,1)S(1)}, bf16[8,4096]{1,0:T(8,128)(2,1)S(1)}) all-reduce(f32[1,128,4096]{2,1,0:T(8,128)} %fusion.15, f32[8,4096]{1,0:T(8,128)S(1)} %fusion.21), channel_id=1, replica_groups=mesh['pair'=1,'tp'=4,'side'=8] {'tp'}, use_global_device_ids=true, to_apply=%region_3.4 | all-reduce | flops 557056 | bytes 3342336 | tf_op jit(solution)/shard_map/psum | solution.py:84
  131.1 18.4 %fusion.31 = bf16[1,128,2,2752]{1,3,2,0:T(8,128)(2,1)S(1)} fusion(bf16[1,2,2752,4096]{3,2,1,0:T(8,128)(2,1)} %param.20, bf16[1,128,4096]{2,1,0:T(8,128)(2,1)S(1)} %get-tuple-element.31, f32[4096]{0:T(1024)S(1)} %bitcast.171, f32[128]{0:T(128)S(1)} %add_rsqrt_fusion.2), kind=kOutput, calls=%fused_computation.25 | convolution fusion | flops 5774163968 | bytes 47563264 | tf_op jit(solution)/shard_map/...d,kfd->...kf/dot_general | solution.py:39
  149.5 9.2 %fusion.18 = f32[1,128,4096]{2,1,0:T(8,128)S(1)} fusion(bf16[1,2752,4096]{2,1,0:T(8,128)(2,1)} %param.21, bf16[1,128,2,2752]{1,3,2,0:T(8,128)(2,1)S(1)} %fusion.31), kind=kOutput, calls=%fused_computation.16 | convolution fusion | flops 2888499200 | bytes 26050560 | tf_op jit(solution)/shard_map/...f,fd->...d/dot_general | solution.py:43
  158.8 18.7 %fusion.34 = bf16[8,2,2752]{2,0,1:T(8,128)(2,1)S(1)} fusion(bf16[1,2,2752,4096]{3,2,1,0:T(8,128)(2,1)} %param.29, bf16[8,4096]{1,0:T(8,128)(2,1)S(1)} %get-tuple-element.29, f32[4096]{0:T(1024)S(1)} %bitcast.175, f32[8]{0:T(128)S(1)} %add_rsqrt_fusion), kind=kOutput, calls=%fused_computation.26 | convolution fusion | flops 360885248 | bytes 45258784 | tf_op jit(solution)/shard_map/...d,kfd->...kf/dot_general | solution.py:39
  177.6 9.0 %fusion.7 = f32[8,4096]{1,0:T(8,128)S(1)} fusion(bf16[1,2752,4096]{2,1,0:T(8,128)(2,1)} %param.30, bf16[8,2,2752]{2,0,1:T(8,128)(2,1)S(1)} %fusion.34), kind=kOutput, calls=%fused_computation.7 | convolution fusion | flops 180531200 | bytes 22763520 | tf_op jit(solution)/shard_map/...f,fd->...d/dot_general | solution.py:43
  186.6 45.2 %all-reduce.5 = (bf16[1,128,4096]{2,1,0:T(8,128)(2,1)}, bf16[8,4096]{1,0:T(8,128)(2,1)S(1)}) all-reduce(f32[1,128,4096]{2,1,0:T(8,128)S(1)} %fusion.18, f32[8,4096]{1,0:T(8,128)S(1)} %fusion.7), channel_id=1, replica_groups=mesh['pair'=1,'tp'=4,'side'=8] {'tp'}, use_global_device_ids=true, to_apply=%region_5.6 | all-reduce | flops 557056 | bytes 3342336 | tf_op jit(solution)/shard_map/psum | solution.py:86
  231.8 2.4 fusion.55
  234.2 1.1 copy.147
  235.7 0.6 fusion.83
  236.4 9.8 %collective-permute-done = bf16[2,32,32,128]{3,2,1,0:T(8,128)(2,1)S(1)} collective-permute-done((bf16[2,32,32,128]{3,2,1,0:T(8,128)(2,1)S(1)}, bf16[2,32,32,128]{3,2,1,0:T(8,128)(2,1)S(1)}, u32[]{:S(2)}, u32[]{:S(2)}) %collective-permute-start) | collective-permute-done | bytes 524320 | tf_op jit(solution)/shard_map/ppermute | solution.py:155
  246.2 1.0 copy.99
  247.2 3.6 %all-to-all-start.1 = ((bf16[2,1,32,8,4,128]{5,2,3,0,1,4:T(8,128)(2,1)}), bf16[2,1,32,8,4,128]{5,2,3,0,1,4:T(8,128)(2,1)S(1)}, u32[]{:S(2)}, u32[]{:S(2)}) async-start(bf16[2,1,32,8,4,128]{5,2,3,0,1,4:T(8,128)(2,1)} %copy.99), calls=%async_computation.1 | async-start | bytes 1048576 | tf_op jit(solution)/shard_map/all_to_all | solution.py:134
  250.7 9.8 %broadcast_select_fusion = (bf16[1,8,256,8,1,128]{5,3,4,2,1,0:T(8,128)(2,1)}, bf16[1,8,256,8,1,128]{5,3,4,2,1,0:T(8,128)(2,1)}) fusion(bf16[1,8,256,8,1,128]{5,3,4,2,1,0:T(8,128)(2,1)} %param.25, pred[8,256]{1,0:T(8,128)(4,1)S(1)} %get-tuple-element.64, bf16[8,8,128]{2,1,0:T(8,128)(2,1)S(1)} %copy.102, bf16[1,8,256,8,1,128]{5,3,4,2,1,0:T(8,128)(2,1)} %param.24, ...), kind=kLoop, calls=%fused_computation.22 | loop fusion | flops 4194304 | bytes 16812032 | tf_op jit(solution)/shard_map/jit(_where)/select_n | solution.py:120
  260.7 0.8 fusion.134
  (55 shorter events, 4.5 us)
Async XLA Ops:
  0.7 31.5 %copy-start.3 = (f32[1,2,4096]{2,1,0:T(2,128)S(1)}, f32[1,2,4096]{2,1,0:T(2,128)}, u32[]{:S(2)}) copy-start(f32[1,2,4096]{2,1,0:T(2,128)} %param.22) | copy-start | bytes 98308
  0.7 31.5 %copy-start = (bf16[128,4096]{1,0:T(8,128)(2,1)S(1)}, bf16[128,4096]{1,0:T(8,128)(2,1)}, u32[]{:S(2)}) copy-start(bf16[128,4096]{1,0:T(8,128)(2,1)} %param.16) | copy-start | bytes 3145732
  44.2 1.1 copy-start.1
  44.2 9.1 %copy-start.5 = (s32[8]{0:T(128)S(1)}, s32[8]{0:T(128)}, u32[]{:S(2)}) copy-start(s32[8]{0:T(128)} %param.26) | copy-start | bytes 100
  47.4 186.9 %all-to-all-start = ((bf16[2,4,32,1,8,128]{5,4,2,3,0,1:T(8,128)(2,1)}), bf16[2,4,32,1,8,128]{5,4,2,3,0,1:T(8,128)(2,1)}, u32[]{:S(2)}, u32[]{:S(2)}) async-start(bf16[2,4,32,1,8,128]{5,4,2,3,0,1:T(8,128)(2,1)} %copy.96), calls=%async_computation | async-start | bytes 1048576 | tf_op jit(solution)/shard_map/all_to_all | solution.py:127
  54.5 6.4 %copy-start.4 = (f32[1,2,4096]{2,1,0:T(2,128)S(1)}, f32[1,2,4096]{2,1,0:T(2,128)}, u32[]{:S(2)}) copy-start(f32[1,2,4096]{2,1,0:T(2,128)} %param.31) | copy-start | bytes 98308
  54.5 6.4 %copy-start.2 = (bf16[8,4096]{1,0:T(8,128)(2,1)S(1)}, bf16[8,4096]{1,0:T(8,128)(2,1)}, u32[]{:S(2)}) copy-start(bf16[8,4096]{1,0:T(8,128)(2,1)} %param.23) | copy-start | bytes 196612
  235.4 10.8 %collective-permute-start = (bf16[2,32,32,128]{3,2,1,0:T(8,128)(2,1)S(1)}, bf16[2,32,32,128]{3,2,1,0:T(8,128)(2,1)S(1)}, u32[]{:S(2)}, u32[]{:S(2)}) collective-permute-start(bf16[2,32,32,128]{3,2,1,0:T(8,128)(2,1)S(1)} %bitcast.169), channel_id=1, source_target_pairs={{0,4},{1,5},{2,6},{3,7},{4,0},{5,1},{6,2},{7,3},{8,12},{9,13},{10,... | collective-permute-start | bytes 1572872 | tf_op jit(solution)/shard_map/ppermute | solution.py:155
  247.2 13.4 %all-to-all-start.1 = ((bf16[2,1,32,8,4,128]{5,2,3,0,1,4:T(8,128)(2,1)}), bf16[2,1,32,8,4,128]{5,2,3,0,1,4:T(8,128)(2,1)S(1)}, u32[]{:S(2)}, u32[]{:S(2)}) async-start(bf16[2,1,32,8,4,128]{5,2,3,0,1,4:T(8,128)(2,1)} %copy.99), calls=%async_computation.1 | async-start | bytes 1048576 | tf_op jit(solution)/shard_map/all_to_all | solution.py:134
where the time goes:
time: 263 us; the launch traced here: 262 us
  matrix products  96.2 us (37%)
  blocking collectives  91.3 us (35%)
  local copies, waits for them, and re-layouts  37.4 us (14%)
  other arithmetic  15.5 us (6%)
  starting transfers between devices  9.82 us (4%)
  waiting for transfers between devices  9.8 us (4%)
    psum x1, blocking collectives, run_prefill(): hidden = add_residual(hidden, lax.psum(part_sum, 'tp').astype(jnp.bfloat16))  46.1 us
    psum x1, blocking collectives, run_prefill(): hidden = add_residual(hidden, lax.psum(mlp_part, 'tp').astype(jnp.bfloat16))  45.2 us
    dot_general x2, matrix products, swiglu(): jnp.einsum('...d,kfd->...kf', normed, w_gu, preferred_element_type=jnp.fl...  37.2 us
    squeeze x1, local copies, waits for them, and re-layouts, run_prefill(): w_qkv[layer_idx]  31.4 us
    dot_general x2, matrix products, swiglu(): jnp.einsum('...f,fd->...d', activated, w_down, preferred_element_type=jnp...  18.2 us
    unnamed x1, matrix products  11.8 us
    dot_general x1, matrix products, run_decode(): jnp.einsum('bd,dkhe->bkhe', normed, wqkv_local[layer_idx], preferred_elem...  11.5 us
    select_n x1, other arithmetic, run_decode(): v_next.append(jnp.where(write_at, v_tok[:, None], v_local[layer_idx]))  9.8 us
  transfers between devices with their start and end apart: 3, of which 1 were waited for; matrix products, arithmetic and copies ran while one was open for 38% of the time, Pallas kernels for 0%

commit v1 on v0

v1 whole, which is shorter than its diff:
```python
import functools

import jax
import jax.numpy as jnp
import numpy as np
from jax import lax
from jax.experimental import pallas as pl
from jax.experimental.pallas import tpu as pltpu
from jax.sharding import PartitionSpec as P

EPSILON = 1e-6
THETA = 10000.0
MASKED = -1e30
D_BLOCK = 512
D_SLOTS = 4
F_BLOCK = 256
F_SLOTS = 3
N_BLOCK = 512
GROUPS = 2
F32 = jnp.float32
BF16 = jnp.bfloat16

MESH = pl.DeviceIdType.MESH

VMEM = pl.BlockSpec(memory_space=pltpu.VMEM)
SMEM = pl.BlockSpec(memory_space=pltpu.SMEM)
HBM = pl.BlockSpec(memory_space=pltpu.HBM)


def dot(lhs, rhs):
    return jnp.dot(lhs, rhs, preferred_element_type=F32)


def dot_nt(lhs, rhs):
    return lax.dot_general(lhs, rhs, (((1,), (1,)), ((), ())), preferred_element_type=F32)


def rms(values, gain):
    inv = lax.rsqrt(jnp.mean(values * values, axis=-1, keepdims=True) + EPSILON)
    return (values * inv * gain).astype(BF16)


def rope_rows(positions, head_dim):
    half = head_dim // 2
    inv_freq = np.power(np.float32(THETA), -np.arange(half, dtype=np.float32) * np.float32(2.0) / np.float32(head_dim)).astype(np.float32)
    angles = np.arange(positions, dtype=np.float32)[:, None] * inv_freq[None, :]
    cos_half = np.cos(angles).astype(np.float32)
    sin_half = np.sin(angles).astype(np.float32)
    return jnp.asarray(np.concatenate([cos_half, cos_half], 1)), jnp.asarray(np.concatenate([-sin_half, sin_half], 1))


def rotate(values, cos_b, sin_b):
    return values * cos_b + pltpu.roll(values, values.shape[-1] // 2, 1) * sin_b


def qkv_product(n_ref, block, at, acc):
    kinds, heads = block.shape[1], block.shape[2]
    nb = n_ref[:, pl.ds(pl.multiple_of(at * D_BLOCK, D_BLOCK), D_BLOCK)]
    for kind in range(kinds):
        by_head = jnp.swapaxes(block[:, kind], 0, 1)
        for p in range(heads // 2):
            pair = jnp.concatenate([by_head[2 * p], by_head[2 * p + 1]], axis=1)
            acc[kind * (heads // 2) + p] += dot(nb, pair)


def remote(src, dst, send_sem, recv_sem, where):
    return pltpu.make_async_remote_copy(src_ref=src, dst_ref=dst, send_sem=send_sem, recv_sem=recv_sem, device_id=where, device_id_type=MESH)


def greet(peers):
    barrier = pltpu.get_barrier_semaphore()
    for peer in peers:
        pl.semaphore_signal(barrier, inc=1, device_id=peer, device_id_type=MESH)


def greeted(peers):
    pl.semaphore_wait(pltpu.get_barrier_semaphore(), len(peers))


class RowReduce:
    def __init__(self, y, refs):
        (self.send_a, self.keep_a, self.send_b, self.keep_b, self.got_a, self.got_b,
         self.mid_a, self.mid_b, self.fin_a, self.fin_b, self.s_sem, self.r_sem) = refs
        self.near = {'tp': lax.bitwise_xor(y, 1)}
        self.wrap = {'tp': lax.bitwise_xor(y, 3)}

    @staticmethod
    def scratch(piece, width):
        part = width // GROUPS
        two, one = pltpu.VMEM((GROUPS, 2, piece, part), F32), pltpu.VMEM((GROUPS, piece, part), F32)
        return [two] * 6 + [one] * 4 + [pltpu.SemaphoreType.DMA((2, 2, GROUPS))] * 2

    def first(self, c):
        return (remote(self.send_a.at[c], self.got_a.at[c], self.s_sem.at[0, 0, c], self.r_sem.at[0, 0, c], self.near),
                remote(self.send_b.at[c], self.got_b.at[c], self.s_sem.at[0, 1, c], self.r_sem.at[0, 1, c], self.wrap))

    def second(self, c):
        return (remote(self.mid_a.at[c], self.fin_a.at[c], self.s_sem.at[1, 0, c], self.r_sem.at[1, 0, c], self.wrap),
                remote(self.mid_b.at[c], self.fin_b.at[c], self.s_sem.at[1, 1, c], self.r_sem.at[1, 1, c], self.near))

    def put(self, part, cols, add):
        q = part.shape[0] // 8
        piece = [part[i * q:(i + 1) * q] for i in range(8)]
        size = self.send_a.shape[-1]
        c = cols.start // size
        at = slice(cols.start - c * size, cols.stop - c * size)
        for ref, one, two in ((self.send_a, 2, 4), (self.keep_a, 0, 6), (self.send_b, 7, 5), (self.keep_b, 1, 3)):
            for row, i in ((0, one), (1, two)):
                ref[c, row, :, at] = ref[c, row, :, at] + piece[i] if add else piece[i]

    def start(self, c):
        for copy in self.first(c):
            copy.start()

    def middle(self, c):
        for copy, keep, got, mid, after in zip(self.first(c), (self.keep_a, self.keep_b), (self.got_a, self.got_b), (self.mid_a, self.mid_b), self.second(c)):
            copy.wait_recv()
            mid[c] = keep[c, 1] + got[c, 1]
            after.start()

    def totals(self):
        found = []
        for i, (keep, got, fin) in enumerate(((self.keep_a, self.got_a, self.fin_a), (self.keep_b, self.got_b, self.fin_b))):
            cols = []
            for c in range(GROUPS):
                self.second(c)[i].wait_recv()
                cols.append((keep[c, 0] + got[c, 0]) + fin[c])
            found.append(jnp.concatenate(cols, axis=1))
        return found

    def drain(self):
        for c in range(GROUPS):
            for copy in self.first(c) + self.second(c):
                copy.wait_send()


class RowGather:
    def __init__(self, y, rows, s_sem, r_sem):
        near, wrap = {'tp': lax.bitwise_xor(y, 1)}, {'tp': lax.bitwise_xor(y, 3)}
        moves = ((0, 0, 3, 0, wrap), (0, 1, 1, 1, near), (0, 0, 1, 0, near), (0, 1, 3, 1, wrap), (3, 0, 2, 0, near), (1, 1, 2, 1, wrap))
        self.copies = [remote(rows.at[r, h], rows.at[to, h2], s_sem.at[i], r_sem.at[i], where) for i, (r, h, to, h2, where) in enumerate(moves)]

    @staticmethod
    def scratch(piece, width):
        return [pltpu.VMEM((4, 2, piece, width), BF16)] + [pltpu.SemaphoreType.DMA((6,))] * 2

    def start(self):
        for copy in self.copies[:4]:
            copy.start()

    def forward(self):
        for i in range(2):
            self.copies[i].wait_recv()
            self.copies[4 + i].start()

    def finish(self):
        for copy in self.copies[2:]:
            copy.wait_recv()
        for copy in self.copies:
            copy.wait_send()


class ColumnSum:
    def __init__(self, y, refs):
        self.y = y
        self.part, self.got, self.total, self.s_sem, self.r_sem = refs

    @staticmethod
    def scratch(batch, quarter):
        return [pltpu.VMEM((4, batch, quarter), F32), pltpu.VMEM((4, batch, quarter), F32), pltpu.VMEM((4, batch, quarter), BF16)] + [pltpu.SemaphoreType.DMA((2, 4))] * 2

    def copies(self, step):
        src, dst = ((self.part, self.got), (self.total, self.total))[step]
        return [remote(src.at[0 if step else r], dst.at[r], self.s_sem.at[step, r], self.r_sem.at[step, r], {'tp': lax.bitwise_xor(self.y, r)}) for r in (1, 2, 3)]

    def start(self):
        for copy in self.copies(0):
            copy.start()

    def middle(self):
        for copy in self.copies(0):
            copy.wait_recv()
        self.total[0] = ((self.part[0] + self.got[1]) + (self.got[2] + self.got[3])).astype(BF16)
        for copy in self.copies(1):
            copy.start()

    def finish(self, out_ref):
        for copy in self.copies(1):
            copy.wait_recv()
        quarter = self.total.shape[-1]
        for r in range(4):
            owner = lax.bitwise_xor(self.y, r)
            out_ref[:, pl.ds(pl.multiple_of(owner * quarter, quarter), quarter)] = self.total[r].astype(out_ref.dtype)
        for step in range(2):
            for copy in self.copies(step):
                copy.wait_send()


def attn_kernel(side, s_len, c_len, x_ref, g_ref, cos_ref, sin_ref, tok_ref, dg_ref, wp_hbm, wop_hbm, wd_hbm, kc_hbm, vc_hbm, wod_hbm,
                h_ref, n_out, a_ref, kt_ref, vt_ref, kp_ref, vp_ref,
                buf, sem, wo_buf, wo_sem, cache, cache_sem, n_ref, acc, ctx, ctx_rel, k_scr, v_scr, nd_ref, accd, q_scr, ctxd, part_scr,
                kv_send, kv_got, kv_ssem, kv_rsem, *comm):
    y = lax.axis_index('tp')
    s = lax.axis_index('side')
    far = lax.rem(s + side // 2, side)
    near_peers = [{'tp': lax.bitwise_xor(y, r)} for r in (1, 2, 3)]
    far_peers = [{'tp': lax.bitwise_xor(y, r), 'side': far} for r in range(4)]
    reduce = RowReduce(y, comm[:12])
    rows_all = comm[12]
    gather = RowGather(y, *comm[12:15])
    small = ColumnSum(y, comm[15:20])
    rows, width = x_ref.shape
    batch = tok_ref.shape[0]
    heads, head = wp_hbm.shape[2], wp_hbm.shape[3]
    pairs = heads // 2
    steps = width // D_BLOCK
    scale = head ** -0.5

    def load(i, w_hbm, slot):
        return pltpu.make_async_copy(w_hbm.at[pl.ds(i * D_BLOCK, D_BLOCK)], buf.at[slot], sem.at[slot])

    def wo_load(which):
        return pltpu.make_async_copy((wop_hbm, wod_hbm)[which], wo_buf.at[which], wo_sem.at[which])

    def cache_load(b, which):
        return pltpu.make_async_copy((kc_hbm, vc_hbm)[which].at[b], cache.at[which, b], cache_sem.at[which, b])

    for i in range(D_SLOTS - 1):
        load(i, wp_hbm, i).start()
    greet(near_peers + far_peers)

    @pl.loop(0, rows // 16)
    def _(i):
        r = pl.ds(pl.multiple_of(i * 16, 16), 16)
        n_ref[r, :] = rms(x_ref[r, :].astype(F32), g_ref[0:1, :])

    acc[...] = jnp.zeros_like(acc)
    accd[...] = jnp.zeros_like(accd)

    @pl.loop(0, steps)
    def _(i):
        j = i + D_SLOTS - 1

        @pl.when(j < steps)
        def _():
            load(j, wp_hbm, lax.rem(j, D_SLOTS)).start()

        @pl.when(j >= steps)
        def _():
            load(j - steps, wd_hbm, lax.rem(j, D_SLOTS)).start()

        @pl.when(i == 3)
        def _():
            wo_load(0).start()

        slot = lax.rem(i, D_SLOTS)
        load(i, wp_hbm, slot).wait()
        qkv_product(n_ref, buf.at[slot], i, acc)

    @pl.loop(0, batch)
    def _(b):
        cache_load(b, 0).start()
        cache_load(b, 1).start()

    cos_b, sin_b = cos_ref[:rows, :], sin_ref[:rows, :]
    row_id = lax.broadcasted_iota(jnp.int32, (rows, rows), 0)
    col_id = lax.broadcasted_iota(jnp.int32, (rows, rows), 1)
    allowed = (col_id <= row_id) & (col_id < s_len[0])

    @pl.loop(0, pairs)
    def _(p):
        pair_ctx = []
        for half in range(2):
            lanes = slice(half * head, (half + 1) * head)
            q = rotate(acc[p, :, lanes], cos_b, sin_b).astype(BF16)
            k = rotate(acc[pairs + p, :, lanes], cos_b, sin_b).astype(BF16)
            v = acc[2 * pairs + p, :, lanes].astype(BF16)
            k_scr[2 * p + half] = k
            v_scr[2 * p + half] = v
            scores = jnp.where(allowed, dot_nt(q, k) * scale, MASKED)
            top = jnp.max(scores, axis=-1, keepdims=True)
            weights = jnp.exp(scores - top)
            prob = (weights / jnp.sum(weights, axis=-1, keepdims=True)).astype(BF16)
            pair_ctx.append(dot(prob, v).astype(BF16))
        ctx[:, pl.ds(pl.multiple_of(p * 2 * head, 2 * head), 2 * head)] = jnp.concatenate(pair_ctx, axis=1)

    greeted(near_peers + far_peers)
    block = rows // 4
    for r in range(4):
        owner = lax.bitwise_xor(y, r)
        ctx_rel[r * block:(r + 1) * block, :] = ctx[pl.ds(pl.multiple_of(owner * block, block), block), :]
        for jj in range(heads // 4):
            kv_send[r, 0, jj] = k_scr[jj * 4 + owner]
            kv_send[r, 1, jj] = v_scr[jj * 4 + owner]
    kv_copies = [remote(kv_send.at[r], kv_got.at[r], kv_ssem.at[r], kv_rsem.at[r], far_peers[r]) for r in range(4)]
    wo_load(0).wait()
    lhs = ctx_rel[...]
    group = width // GROUPS
    for c in range(width // N_BLOCK):
        cols = slice(c * N_BLOCK, (c + 1) * N_BLOCK)
        reduce.put(dot(lhs, wo_buf[0, :, cols]), cols, False)
        if cols.stop % group == 0:
            reduce.start(cols.start // group)
    for copy in kv_copies:
        copy.start()

    wo_load(1).start()
    nd_ref[...] = rms(tok_ref[...].astype(F32), dg_ref[0:1, :])

    @pl.loop(0, steps)
    def _(i):
        j = i + D_SLOTS - 1

        @pl.when(j < steps)
        def _():
            load(j, wd_hbm, lax.rem(j + steps, D_SLOTS)).start()

        slot = lax.rem(i + steps, D_SLOTS)
        load(i, wd_hbm, slot).wait()
        qkv_product(nd_ref, buf.at[slot], i, accd)

        @pl.when(i == 4)
        def _():
            reduce.middle(0)

    cos_d = jnp.concatenate([cos_ref[pl.ds(c_len[b], 1), :] for b in range(batch)], axis=0)
    sin_d = jnp.concatenate([sin_ref[pl.ds(c_len[b], 1), :] for b in range(batch)], axis=0)

    def by_row(kind, turn):
        found = []
        for h in range(heads):
            vals = accd[kind * pairs + h // 2, :, (h % 2) * head:(h % 2 + 1) * head]
            found.append(rotate(vals, cos_d, sin_d) if turn else vals)
        return jnp.swapaxes(jnp.stack(found), 0, 1).astype(BF16)

    q_scr[...] = by_row(0, True)
    kt_ref[...] = by_row(1, True)
    vt_ref[...] = by_row(2, False)
    reduce.middle(1)
    slots = cache.shape[2]
    lane = lax.broadcasted_iota(jnp.int32, (heads, slots), 1)
    mine = lax.bitwise_and(lane, heads - 1) == lax.broadcasted_iota(jnp.int32, (heads, slots), 0)

    @pl.loop(0, batch)
    def _(b):
        cache_load(b, 0).wait()
        cache_load(b, 1).wait()
        q, k_tok, v_tok = q_scr[b], kt_ref[b].astype(F32), vt_ref[b].astype(F32)
        scores = dot_nt(q, cache[0, b]) * scale
        scores = jnp.where(mine & (lane < c_len[b] * heads), scores, MASKED)
        own = jnp.sum(q.astype(F32) * k_tok, axis=-1, keepdims=True) * scale
        top = jnp.maximum(jnp.max(scores, axis=-1, keepdims=True), own)
        weights = jnp.exp(scores - top)
        own_w = jnp.exp(own - top)
        total = jnp.sum(weights, axis=-1, keepdims=True) + own_w
        prob = (weights / total).astype(BF16)
        own_prob = (own_w / total).astype(BF16).astype(F32)
        ctxd[b] = (dot(prob, cache[1, b]) + own_prob * v_tok).astype(BF16).astype(F32)

    by_head = jnp.swapaxes(ctxd[...], 0, 1)
    lhs_d = jnp.concatenate([by_head[h] for h in range(heads)], axis=1).astype(BF16)
    wo_load(1).wait()
    quarter = width // 4
    for c in range(4):
        part_scr[c] = dot(lhs_d, wo_buf[1, :, c * quarter:(c + 1) * quarter])
    for r in range(4):
        small.part[r] = part_scr[lax.bitwise_xor(y, r)]
    small.start()

    piece = block // 2
    for at, total in zip((0, 1), reduce.totals()):
        x_rows = x_ref[pl.ds(pl.multiple_of(y * block + at * piece, piece), piece), :]
        h = (x_rows.astype(F32) + total.astype(BF16).astype(F32)).astype(BF16)
        h_ref[at * piece:(at + 1) * piece, :] = h
        rows_all[0, at] = rms(h.astype(F32), g_ref[1:2, :])
    gather.start()
    small.middle()
    for r in range(4):
        kv_copies[r].wait_recv()
        owner = lax.bitwise_xor(y, r)
        for jj in range(heads // 4):
            k_scr[owner * (heads // 4) + jj] = kv_got[r, 0, jj]
            v_scr[owner * (heads // 4) + jj] = kv_got[r, 1, jj]
    kp_ref[...] = jnp.swapaxes(k_scr[...], 0, 1)
    vp_ref[...] = jnp.swapaxes(v_scr[...], 0, 1)
    gather.forward()
    small.finish(a_ref)
    reduce.drain()
    for copy in kv_copies:
        copy.wait_send()
    gather.finish()
    n_out[...] = rows_all[...]


def mlp_kernel(n_all, own_ref, tok_ref, a_ref, dg_ref, gup_hbm, dnp_hbm, gud_hbm, dnd_hbm, h_out, d_out,
               g_buf, u_buf, d_buf, sem, n_ref, nd_ref, hd_ref, part_scr, *comm):
    y = lax.axis_index('tp')
    peers = [{'tp': lax.bitwise_xor(y, r)} for r in (1, 2, 3)]
    reduce = RowReduce(y, comm[:12])
    rows_all = comm[12]
    gather = RowGather(y, *comm[12:15])
    small = ColumnSum(y, comm[15:20])
    ff, width = dnp_hbm.shape
    steps = pl.cdiv(ff, F_BLOCK)
    quarter = width // 4

    def at(i):
        return pl.multiple_of(jnp.minimum(i * F_BLOCK, ff - F_BLOCK), 8)

    def loads(i, gu_hbm, down_hbm, slot):
        rows = pl.ds(at(i), F_BLOCK)
        return (pltpu.make_async_copy(gu_hbm.at[0, rows], g_buf.at[slot], sem.at[0, slot]),
                pltpu.make_async_copy(gu_hbm.at[1, rows], u_buf.at[slot], sem.at[1, slot]),
                pltpu.make_async_copy(down_hbm.at[rows], d_buf.at[slot], sem.at[2, slot]))

    def product(i, slot, n, add):
        gate = dot_nt(n, g_buf[slot]).astype(BF16).astype(F32)
        up = dot_nt(n, u_buf[slot]).astype(BF16).astype(F32)
        m = jax.nn.silu(gate) * up
        lane = lax.broadcasted_iota(jnp.int32, m.shape, 1)
        m = jnp.where(at(i) + lane >= i * F_BLOCK, m, 0.0).astype(BF16)
        for c in range(width // N_BLOCK):
            cols = slice(c * N_BLOCK, (c + 1) * N_BLOCK)
            add(dot(m, d_buf[slot, :, cols]), cols)

    for i in range(F_SLOTS - 1):
        for copy in loads(i, gup_hbm, dnp_hbm, i):
            copy.start()
    greet(peers)
    rows = n_ref.shape[0]
    piece = rows // 8
    for r in range(4):
        for half in range(2):
            i = (2 * r + half) * piece
            n_ref[i:i + piece, :] = n_all[r, half]
    for ref in (reduce.send_a, reduce.keep_a, reduce.send_b, reduce.keep_b, part_scr):
        ref[...] = jnp.zeros_like(ref)
    h_dec = (tok_ref[...].astype(F32) + a_ref[...].astype(F32)).astype(BF16)
    hd_ref[...] = h_dec.astype(F32)
    nd_ref[...] = rms(hd_ref[...], dg_ref[1:2, :])

    @pl.loop(0, steps)
    def _(i):
        j = i + F_SLOTS - 1

        @pl.when(j < steps)
        def _():
            for copy in loads(j, gup_hbm, dnp_hbm, lax.rem(j, F_SLOTS)):
                copy.start()

        @pl.when(j >= steps)
        def _():
            for copy in loads(j - steps, gud_hbm, dnd_hbm, lax.rem(j, F_SLOTS)):
                copy.start()

        slot = lax.rem(i, F_SLOTS)
        for copy in loads(i, gup_hbm, dnp_hbm, slot):
            copy.wait()
        product(i, slot, n_ref[...], lambda part, cols: reduce.put(part, cols, True))

    greeted(peers)
    for c in range(GROUPS):
        reduce.start(c)

    def add_dec(part, cols):
        c = cols.start // quarter
        part_scr[c, :, cols.start - c * quarter:cols.stop - c * quarter] += part

    def own_rows():
        for half, total in zip((0, 1), reduce.totals()):
            h = own_ref[half * piece:(half + 1) * piece, :].astype(F32)
            rows_all[0, half] = (h + total.astype(BF16).astype(F32)).astype(BF16)
        gather.start()

    @pl.loop(0, steps)
    def _(i):
        j = i + F_SLOTS - 1

        @pl.when(j < steps)
        def _():
            for copy in loads(j, gud_hbm, dnd_hbm, lax.rem(j + steps, F_SLOTS)):
                copy.start()

        slot = lax.rem(i + steps, F_SLOTS)
        for copy in loads(i, gud_hbm, dnd_hbm, slot):
            copy.wait()
        product(i, slot, nd_ref[...], add_dec)

        @pl.when(i == 2)
        def _():
            reduce.middle(0)

        @pl.when(i == 5)
        def _():
            reduce.middle(1)

        @pl.when(i == 8)
        def _():
            own_rows()

    for r in range(4):
        small.part[r] = part_scr[lax.bitwise_xor(y, r)]
    small.start()
    gather.forward()
    small.middle()
    small.finish(nd_ref)
    d_out[...] = (hd_ref[...] + nd_ref[...].astype(F32)).astype(BF16)
    reduce.drain()
    gather.finish()
    for r in range(4):
        owner = lax.bitwise_xor(y, r)
        for half in range(2):
            h_out[pl.ds(pl.multiple_of((2 * owner + half) * piece, piece), piece), :] = rows_all[r, half]


def cache_kernel(c_len, kt_ref, vt_ref, kc_hbm, vc_hbm, kn_hbm, vn_hbm, cache, in_sem, out_sem):
    batch = kt_ref.shape[0]

    def load(b, which):
        return pltpu.make_async_copy((kc_hbm, vc_hbm)[which].at[b], cache.at[which, b], in_sem.at[which, b])

    def store(b, which):
        return pltpu.make_async_copy(cache.at[which, b], (kn_hbm, vn_hbm)[which].at[b], out_sem.at[which, b])

    @pl.loop(0, batch)
    def _(b):
        load(b, 0).start()
        load(b, 1).start()

    @pl.loop(0, batch)
    def _(b):
        for which, tok in ((0, kt_ref), (1, vt_ref)):
            load(b, which).wait()
            cache[which, b, c_len[b]] = tok[b]
            store(b, which).start()

    @pl.loop(0, batch)
    def _(b):
        store(b, 0).wait()
        store(b, 1).wait()


def call(kernel, name, in_specs, out_specs, out_shape, scratch, us, collective_id=None):
    return pl.pallas_call(kernel, name=name, in_specs=in_specs, out_specs=out_specs, out_shape=out_shape, scratch_shapes=scratch,
                          cost_estimate=pl.CostEstimate(flops=int(us * 2e7), bytes_accessed=int(us * 3e6), transcendentals=0),
                          compiler_params=pltpu.CompilerParams(vmem_limit_bytes=62 * 2 ** 20, collective_id=collective_id, has_side_effects=collective_id is not None))


def shape(dims, dtype=F32):
    return jax.ShapeDtypeStruct(dims, dtype)


def solution(mesh):
    side = mesh.shape['side']
    inst_axes = ('pair', 'side')
    rows_spec = P(inst_axes, None)
    vec_spec = P(inst_axes)
    cache_spec = P(None, inst_axes, None, None, 'tp', None)
    prompt_spec = P(None, inst_axes, None, 'tp', None)
    in_specs = (rows_spec, vec_spec, P(None, None, None, 'tp', None), P(None, 'tp', None, None), P(None, None, 'tp', None), P(None, 'tp', None), P(None, None, None), rows_spec, cache_spec, cache_spec, vec_spec, P(None, None, None, None, 'tp', None), P(None, None, 'tp', None, None), P(None, None, 'tp', None), P(None, 'tp', None), P(None, None, None))
    out_specs = (rows_spec, rows_spec, prompt_spec, prompt_spec, cache_spec, cache_spec)

    def device_fn(prompt_x, s_len, w_qkv_pre, w_out_pre, w_gu_pre, w_down_pre, gain_pre, dec_tokens, k_cache, v_cache, c_len, w_qkv_dec, w_out_dec, w_gu_dec, w_down_dec, gain_dec):
        rows, width = prompt_x.shape
        batch = dec_tokens.shape[0]
        heads, head = w_qkv_pre.shape[3], w_qkv_pre.shape[4]
        cache_len = k_cache.shape[2]
        piece = rows // 8
        quarter = width // 4
        pairs = heads // 2
        dma = pltpu.SemaphoreType.DMA
        cos_tab, sin_tab = rope_rows(max(rows, cache_len), head)
        comm = RowReduce.scratch(piece, width) + RowGather.scratch(piece, width) + ColumnSum.scratch(batch, quarter)
        flat = (batch, cache_len * heads, head)
        wide = (batch, cache_len, heads, head)
        kv_block = pltpu.VMEM((4, 2, heads // 4, rows, head), BF16)
        h_own, n_all, a_all, k_tok, v_tok, k_prompt, v_prompt = call(
            functools.partial(attn_kernel, side), 'attn', [SMEM] * 2 + [VMEM] * 6 + [HBM] * 6, [VMEM] * 7,
            [shape((2 * piece, width), BF16), shape((4, 2, piece, width), BF16), shape((batch, width), BF16)] + [shape((batch, heads, head), BF16)] * 2 + [shape((rows, heads, head), BF16)] * 2,
            [pltpu.VMEM((D_SLOTS, D_BLOCK, 3, heads, head), BF16), dma((D_SLOTS,)), pltpu.VMEM((2, heads * head, width), BF16), dma((2,)),
             pltpu.VMEM((2,) + flat, BF16), dma((2, batch)),
             pltpu.VMEM((rows, width), BF16), pltpu.VMEM((3 * pairs, rows, 2 * head), F32), pltpu.VMEM((rows, heads * head), BF16), pltpu.VMEM((rows, heads * head), BF16),
             pltpu.VMEM((heads, rows, head), BF16), pltpu.VMEM((heads, rows, head), BF16),
             pltpu.VMEM((batch, width), BF16), pltpu.VMEM((3 * pairs, batch, 2 * head), F32), pltpu.VMEM((batch, heads, head), BF16), pltpu.VMEM((batch, heads, head), F32), pltpu.VMEM((4, batch, quarter), F32),
             kv_block, kv_block, dma((4,)), dma((4,))] + comm, 46, 0)(
            s_len, c_len, prompt_x, gain_pre[0], cos_tab, sin_tab, dec_tokens, gain_dec[0],
            w_qkv_pre[0], w_out_pre.reshape(heads * head, width), w_qkv_dec.reshape(width, 3, heads, head),
            k_cache.reshape(flat), v_cache.reshape(flat), w_out_dec.reshape(heads * head, width))
        h_out, dec_out = call(
            mlp_kernel, 'mlp', [VMEM] * 5 + [HBM] * 4, [VMEM] * 2, [shape((rows, width), BF16), shape((batch, width), BF16)],
            [pltpu.VMEM((F_SLOTS, F_BLOCK, width), BF16)] * 3 + [dma((3, F_SLOTS)), pltpu.VMEM((rows, width), BF16), pltpu.VMEM((batch, width), BF16), pltpu.VMEM((batch, width), F32), pltpu.VMEM((4, batch, quarter), F32)] + comm, 50, 1)(
            n_all, h_own, dec_tokens, a_all, gain_dec[0], w_gu_pre[0], w_down_pre[0], w_gu_dec[0], w_down_dec[0])
        k_new, v_new = call(
            cache_kernel, 'cache', [SMEM] + [VMEM] * 2 + [HBM] * 2, [HBM] * 2, [shape(wide, BF16)] * 2,
            [pltpu.VMEM((2,) + wide, BF16), dma((2, batch)), dma((2, batch))], 7)(c_len, k_tok, v_tok, k_cache.reshape(wide), v_cache.reshape(wide))
        prompt_shape = (1, rows, heads, 1, head)
        return h_out, dec_out, k_prompt.reshape(prompt_shape), v_prompt.reshape(prompt_shape), k_new.reshape(k_cache.shape), v_new.reshape(v_cache.shape)

    return jax.shard_map(device_fn, mesh=mesh, in_specs=in_specs, out_specs=out_specs, check_vma=False)
```

time: 263 us -> 134 us (0.51)
  Pallas kernels: 0 us -> 127 us
  matrix products: 96.2 us -> 0 us
  blocking collectives: 91.3 us -> 0 us
  local copies, waits for them, and re-layouts: 37.4 us -> 5.17 us
  other arithmetic: 15.5 us -> 0 us
  starting transfers between devices: 9.82 us -> 0 us
  waiting for transfers between devices: 9.8 us -> 0 us
    pallas_call x0 -> x3, Pallas kernels: none -> 127 us  [the longest x1 61 us: device_fn(): call(functools.partial(attn_kernel, side), 'attn', [SMEM] * 2 + [VMEM] *...]
    psum x2 -> x0, blocking collectives: 91.3 us -> none  [the longest x1 46.1 us: run_prefill(): hidden = add_residual(hidden, lax.psum(part_sum, 'tp').astype(jnp.bfloat16))]
    dot_general x9 -> x0, matrix products: 84 us -> none  [the longest x2 37.2 us: swiglu(): jnp.einsum('...d,kfd->...kf', normed, w_gu, preferred_element_type=jnp.fl...]
    squeeze x3 -> x0, local copies, waits for them, and re-layouts: 31.5 us -> none  [the longest x1 31.4 us: run_prefill(): w_qkv[layer_idx]]
    unnamed x1 -> x0, matrix products: 11.8 us -> none
    select_n x1 -> x0, other arithmetic: 9.8 us -> none  [run_decode(): v_next.append(jnp.where(write_at, v_tok[:, None], v_local[layer_idx]))]
    ppermute x1 -> x0, waiting for transfers between devices: 9.8 us -> none  [device_fn(): kv_rows = lax.ppermute(kv_rows, 'side', partner_perm)]
    all_to_all x2 -> x0, starting transfers between devices: 9.49 us -> none  [the longest x1 5.93 us: heads_to_rows(): gathered = lax.all_to_all(by_block, 'tp', 1, 2)]
  transfers between devices with their start and end apart: 3 -> 0, of which waited for: 1 -> 0; matrix products, arithmetic and copies ran while one was open for 38% -> 0% of each run, Pallas kernels for 0% -> 0%
where the time goes in v1:
time: 134 us; the launch traced here: 133 us
  Pallas kernels  127 us (95%)
  local copies, waits for them, and re-layouts  5.17 us (4%)
    pallas_call x1, Pallas kernels, device_fn(): call(functools.partial(attn_kernel, side), 'attn', [SMEM] * 2 + [VMEM] *...  61 us
    pallas_call x1, Pallas kernels, device_fn(): call(mlp_kernel, 'mlp', [VMEM] * 5 + [HBM] * 4, [VMEM] * 2, [shape((rows,...  58.6 us
    pallas_call x1, Pallas kernels, device_fn(): call(cache_kernel, 'cache', [SMEM] + [VMEM] * 2 + [HBM] * 2, [HBM] * 2, [...  7.31 us
    unnamed x8, local copies, waits for them, and re-layouts  5.17 us

profile of v1, /device:TPU:100, one launch (start us, length us, event | category | flops | bytes accessed | tf_op | source)
XLA Modules:
  0.0 133.4 jit_solution(7514616710385184602)
XLA Ops:
  1.3 61.0 %attn.1 = (bf16[32,4096]{1,0:T(8,128)(2,1)}, bf16[4,2,16,4096]{3,2,1,0:T(8,128)(2,1)}, bf16[8,4096]{1,0:T(8,128)(2,1)}, bf16[8,8,128]{2,1,0:T(8,128)(2,1)}, bf16...) custom-call(s32[1]{0:T(128)S(6)} %copy.32.s_len, s32[8]{0:T(128)} %c_len.3, ...), custom_call_target="tpu_custom_call" | custom-call | flops 920000000 | bytes 138000000 | tf_op jit(solution)/shard_map/attn/pallas_call | solution.py:577
  62.2 0.0 copy-start.1
  62.3 0.0 copy-start
  62.3 58.6 %mlp.1 = (bf16[128,4096]{1,0:T(8,128)(2,1)}, bf16[8,4096]{1,0:T(8,128)(2,1)}) custom-call(bf16[4,2,16,4096]{3,2,1,0:T(8,128)(2,1)} %get-tuple-element.17.n_all, bf16[32,4096]{1,0:T(8,128)(2,1)} %get-tuple-element.18.own_ref, bf16[8,4096]{1,0:T(8,128)(2,1)} %tok_ref.3, bf16[8,4096]{1,0:T(8,128)(2,1)} %get-tuple-element.19.a_ref, f32[2,4096]{1,0:T(2,128)} %bitcast.41, ...), custom_call_target="tpu_custom_call" | custom-call | flops 1000000000 | bytes 150000000 | tf_op jit(solution)/shard_map/mlp/pallas_call | solution.py:589
  120.9 7.3 %cache.1 = (bf16[8,256,8,128]{3,2,1,0:T(8,128)(2,1)}, bf16[8,256,8,128]{3,2,1,0:T(8,128)(2,1)}) custom-call(s32[8]{0:T(128)} %c_len.3, bf16[8,8,128]{2,1,0:T(8,128)(2,1)} %get-tuple-element.24.kt_ref, bf16[8,8,128]{2,1,0:T(8,128)(2,1)} %get-tuple-element.25.vt_ref, bf16[8,256,8,128]{3,2,1,0:T(8,128)(2,1)} %bitcast.33, bf16[8,256,8,128]{3,2,1,0:T(8,128)(2,1)} %bitcast.35), custom_call_target="tpu_custom_call" | custom-call | flops 140000000 | bytes 21000000 | tf_op jit(solution)/shard_map/cache/pallas_call | solution.py:593
  128.2 2.3 %copy.33 = bf16[128,4096]{1,0:T(8,128)(2,1)} copy(bf16[128,4096]{1,0:T(8,128)(2,1)} %get-tuple-element.40) | data formatting | bytes 2097152
  130.5 1.5 %copy.34 = bf16[8,4096]{1,0:T(8,128)(2,1)} copy(bf16[8,4096]{1,0:T(8,128)(2,1)} %get-tuple-element.41) | data formatting | bytes 131072
  132.0 0.0 copy-done.1
  132.0 0.7 copy.35
  132.7 0.0 copy-done
  132.7 0.7 copy.36
Async XLA Ops:
  62.2 69.7 %copy-start.1 = (bf16[128,8,128]{2,1,0:T(8,128)(2,1)S(1)}, bf16[128,8,128]{2,1,0:T(8,128)(2,1)}, u32[]{:S(2)}) copy-start(bf16[128,8,128]{2,1,0:T(8,128)(2,1)} %get-tuple-element.22) | copy-start | bytes 786436
  62.3 70.4 %copy-start = (bf16[128,8,128]{2,1,0:T(8,128)(2,1)S(1)}, bf16[128,8,128]{2,1,0:T(8,128)(2,1)}, u32[]{:S(2)}) copy-start(bf16[128,8,128]{2,1,0:T(8,128)(2,1)} %get-tuple-element.23) | copy-start | bytes 786436

commit v2 on v1

--- a/solution.py
+++ b/solution.py
@@ -12,9 +12,11 @@
 THETA = 10000.0
 MASKED = -1e30
 D_BLOCK = 512
-D_SLOTS = 4
+D_SLOTS = 3
 F_BLOCK = 256
-F_SLOTS = 3
+F_SLOTS = 4
+LATE_SLOTS = 6
+ROW_SLOTS = 4
 N_BLOCK = 512
 GROUPS = 2
 F32 = jnp.float32
@@ -94,9 +96,12 @@
         return (remote(self.send_a.at[c], self.got_a.at[c], self.s_sem.at[0, 0, c], self.r_sem.at[0, 0, c], self.near),
                 remote(self.send_b.at[c], self.got_b.at[c], self.s_sem.at[0, 1, c], self.r_sem.at[0, 1, c], self.wrap))
 
+    def second_of(self, i, c):
+        mid, fin, where = ((self.mid_a, self.fin_a, self.wrap), (self.mid_b, self.fin_b, self.near))[i]
+        return remote(mid.at[c], fin.at[c], self.s_sem.at[1, i, c], self.r_sem.at[1, i, c], where)
+
     def second(self, c):
-        return (remote(self.mid_a.at[c], self.fin_a.at[c], self.s_sem.at[1, 0, c], self.r_sem.at[1, 0, c], self.wrap),
-                remote(self.mid_b.at[c], self.fin_b.at[c], self.s_sem.at[1, 1, c], self.r_sem.at[1, 1, c], self.near))
+        return self.second_of(0, c), self.second_of(1, c)
 
     def put(self, part, cols, add):
         q = part.shape[0] // 8
@@ -118,14 +123,11 @@
             mid[c] = keep[c, 1] + got[c, 1]
             after.start()
 
-    def totals(self):
+    def totals(self, c):
         found = []
         for i, (keep, got, fin) in enumerate(((self.keep_a, self.got_a, self.fin_a), (self.keep_b, self.got_b, self.fin_b))):
-            cols = []
-            for c in range(GROUPS):
-                self.second(c)[i].wait_recv()
-                cols.append((keep[c, 0] + got[c, 0]) + fin[c])
-            found.append(jnp.concatenate(cols, axis=1))
+            self.second_of(i, c).wait_recv()
+            found.append((keep[c, 0] + got[c, 0]) + fin[c])
         return found
 
     def drain(self):
@@ -138,26 +140,31 @@
     def __init__(self, y, rows, s_sem, r_sem):
         near, wrap = {'tp': lax.bitwise_xor(y, 1)}, {'tp': lax.bitwise_xor(y, 3)}
         moves = ((0, 0, 3, 0, wrap), (0, 1, 1, 1, near), (0, 0, 1, 0, near), (0, 1, 3, 1, wrap), (3, 0, 2, 0, near), (1, 1, 2, 1, wrap))
-        self.copies = [remote(rows.at[r, h], rows.at[to, h2], s_sem.at[i], r_sem.at[i], where) for i, (r, h, to, h2, where) in enumerate(moves)]
+        part = rows.shape[-1] // GROUPS
+        self.copies = []
+        for c in range(GROUPS):
+            at = pl.ds(c * part, part)
+            self.copies.append([functools.partial(remote, rows.at[r, h, :, at], rows.at[to, h2, :, at], s_sem.at[c, i], r_sem.at[c, i], where) for i, (r, h, to, h2, where) in enumerate(moves)])
 
     @staticmethod
     def scratch(piece, width):
-        return [pltpu.VMEM((4, 2, piece, width), BF16)] + [pltpu.SemaphoreType.DMA((6,))] * 2
-
-    def start(self):
-        for copy in self.copies[:4]:
-            copy.start()
-
-    def forward(self):
+        return [pltpu.VMEM((4, 2, piece, width), BF16)] + [pltpu.SemaphoreType.DMA((GROUPS, 6))] * 2
+
+    def start(self, c):
+        for copy in self.copies[c][:4]:
+            copy().start()
+
+    def forward(self, c):
         for i in range(2):
-            self.copies[i].wait_recv()
-            self.copies[4 + i].start()
+            self.copies[c][i]().wait_recv()
+            self.copies[c][4 + i]().start()
 
     def finish(self):
-        for copy in self.copies[2:]:
-            copy.wait_recv()
-        for copy in self.copies:
-            copy.wait_send()
+        for c in range(GROUPS):
+            for copy in self.copies[c][2:]:
+                copy().wait_recv()
+            for copy in self.copies[c]:
+                copy().wait_send()
 
 
 class ColumnSum:
@@ -196,10 +203,10 @@
                 copy.wait_send()
 
 
-def attn_kernel(side, s_len, c_len, x_ref, g_ref, cos_ref, sin_ref, tok_ref, dg_ref, wp_hbm, wop_hbm, wd_hbm, kc_hbm, vc_hbm, wod_hbm,
-                h_ref, n_out, a_ref, kt_ref, vt_ref, kp_ref, vp_ref,
-                buf, sem, wo_buf, wo_sem, cache, cache_sem, n_ref, acc, ctx, ctx_rel, k_scr, v_scr, nd_ref, accd, q_scr, ctxd, part_scr,
-                kv_send, kv_got, kv_ssem, kv_rsem, *comm):
+def layer_kernel(side, s_len, c_len, g_ref, cos_ref, sin_ref, tok_ref, dg_ref, x_hbm, wp_hbm, wop_hbm, wd_hbm, kc_hbm, vc_hbm, wod_hbm, gup_hbm, dnp_hbm, gud_hbm, dnd_hbm,
+                 h_out, d_out, kt_ref, vt_ref, kp_ref, vp_ref,
+                 x_ref, x_sem, buf, sem, ring, ring_sem, wo_sem, cache, cache_sem, n_ref, acc, ctx, ctx_rel, k_scr, v_scr, nd_ref, hd_ref, accd, q_scr, ctxd, part_scr, own_ref, m_ref, md_ref, late, late_sem,
+                 kv_send, kv_got, kv_ssem, kv_rsem, *comm):
     y = lax.axis_index('tp')
     s = lax.axis_index('side')
     far = lax.rem(s + side // 2, side)
@@ -214,29 +221,74 @@
     heads, head = wp_hbm.shape[2], wp_hbm.shape[3]
     pairs = heads // 2
     steps = width // D_BLOCK
+    ff = dnp_hbm.shape[0]
+    f_steps = pl.cdiv(ff, F_BLOCK)
+    wo_parts = heads * head // F_BLOCK
     scale = head ** -0.5
+    group = width // GROUPS
 
     def load(i, w_hbm, slot):
         return pltpu.make_async_copy(w_hbm.at[pl.ds(i * D_BLOCK, D_BLOCK)], buf.at[slot], sem.at[slot])
 
     def wo_load(which):
-        return pltpu.make_async_copy((wop_hbm, wod_hbm)[which], wo_buf.at[which], wo_sem.at[which])
+        return pltpu.make_async_copy((wop_hbm, wod_hbm)[which], ring.at[pl.ds(which * wo_parts, wo_parts)], wo_sem.at[which])
+
+    def f_at(i):
+        return pl.multiple_of(jnp.minimum(i * F_BLOCK, ff - F_BLOCK), 8)
+
+    def f_slot(i):
+        return lax.rem(i + F_SLOTS - 1, F_SLOTS)
+
+    def gu_loads(t, gu_hbm, i):
+        at, slot = pl.ds(f_at(i), F_BLOCK), f_slot(t)
+        return [pltpu.make_async_copy(gu_hbm.at[which, at], ring.at[3 * slot + which], ring_sem.at[which, slot]) for which in range(2)]
+
+    def down_load(t, down_hbm, i, size):
+        slot = f_slot(t)
+        return pltpu.make_async_copy(down_hbm.at[pl.ds(f_at(i), F_BLOCK), pl.ds(0, size)], ring.at[3 * slot + 2, :, pl.ds(0, size)], ring_sem.at[2, slot])
+
+    def f_start(t):
+        @pl.when(t < f_steps)
+        def _():
+            for copy in gu_loads(t, gup_hbm, t):
+                copy.start()
+
+        @pl.when((t >= f_steps) & (t < 2 * f_steps))
+        def _():
+            for copy in gu_loads(t, gud_hbm, t - f_steps):
+                copy.start()
+
+        @pl.when((t > 0) & (t <= f_steps))
+        def _():
+            down_load(t, dnp_hbm, t - 1, group).start()
+
+        @pl.when((t > f_steps) & (t <= 2 * f_steps))
+        def _():
+            down_load(t, dnd_hbm, t - 1 - f_steps, width).start()
 
     def cache_load(b, which):
-        return pltpu.make_async_copy((kc_hbm, vc_hbm)[which].at[b], cache.at[which, b], cache_sem.at[which, b])
-
-    for i in range(D_SLOTS - 1):
+        slot = lax.rem(b, ROW_SLOTS)
+        return pltpu.make_async_copy((kc_hbm, vc_hbm)[which].at[b], cache.at[which, slot], cache_sem.at[which, slot])
+
+    def late_load(i):
+        slot = lax.rem(i, LATE_SLOTS)
+        return pltpu.make_async_copy(dnp_hbm.at[pl.ds(f_at(i), F_BLOCK), pl.ds(group, group)], late.at[slot], late_sem.at[slot])
+
+    x_copy = pltpu.make_async_copy(x_hbm, x_ref, x_sem)
+    x_copy.start()
+    load(0, wp_hbm, 0).start()
+    greet(near_peers + far_peers)
+    acc[...] = jnp.zeros_like(acc)
+    accd[...] = jnp.zeros_like(accd)
+    x_copy.wait()
+    for i in range(1, D_SLOTS - 1):
         load(i, wp_hbm, i).start()
-    greet(near_peers + far_peers)
 
     @pl.loop(0, rows // 16)
     def _(i):
         r = pl.ds(pl.multiple_of(i * 16, 16), 16)
         n_ref[r, :] = rms(x_ref[r, :].astype(F32), g_ref[0:1, :])
 
-    acc[...] = jnp.zeros_like(acc)
-    accd[...] = jnp.zeros_like(accd)
-
     @pl.loop(0, steps)
     def _(i):
         j = i + D_SLOTS - 1
@@ -249,15 +301,23 @@
         def _():
             load(j - steps, wd_hbm, lax.rem(j, D_SLOTS)).start()
 
+        @pl.when(i == 1)
+        def _():
+            wo_load(0).start()
+
         @pl.when(i == 3)
         def _():
-            wo_load(0).start()
+            wo_load(1).start()
+
+        @pl.when(i == 5)
+        def _():
+            f_start(0)
 
         slot = lax.rem(i, D_SLOTS)
         load(i, wp_hbm, slot).wait()
         qkv_product(n_ref, buf.at[slot], i, acc)
 
-    @pl.loop(0, batch)
+    @pl.loop(0, ROW_SLOTS)
     def _(b):
         cache_load(b, 0).start()
         cache_load(b, 1).start()
@@ -294,17 +354,21 @@
             kv_send[r, 1, jj] = v_scr[jj * 4 + owner]
     kv_copies = [remote(kv_send.at[r], kv_got.at[r], kv_ssem.at[r], kv_rsem.at[r], far_peers[r]) for r in range(4)]
     wo_load(0).wait()
+
+    def wo_product(lhs, which, cols):
+        found = None
+        for i in range(wo_parts):
+            part = dot(lhs[:, i * F_BLOCK:(i + 1) * F_BLOCK], ring[which * wo_parts + i, :, cols])
+            found = part if found is None else found + part
+        return found
+
     lhs = ctx_rel[...]
-    group = width // GROUPS
     for c in range(width // N_BLOCK):
         cols = slice(c * N_BLOCK, (c + 1) * N_BLOCK)
-        reduce.put(dot(lhs, wo_buf[0, :, cols]), cols, False)
+        reduce.put(wo_product(lhs, 0, cols), cols, False)
         if cols.stop % group == 0:
             reduce.start(cols.start // group)
-    for copy in kv_copies:
-        copy.start()
-
-    wo_load(1).start()
+    f_start(1)
     nd_ref[...] = rms(tok_ref[...].astype(F32), dg_ref[0:1, :])
 
     @pl.loop(0, steps)
@@ -319,7 +383,7 @@
         load(i, wd_hbm, slot).wait()
         qkv_product(nd_ref, buf.at[slot], i, accd)
 
-        @pl.when(i == 4)
+        @pl.when(i == 5)
         def _():
             reduce.middle(0)
 
@@ -336,17 +400,21 @@
     q_scr[...] = by_row(0, True)
     kt_ref[...] = by_row(1, True)
     vt_ref[...] = by_row(2, False)
-    reduce.middle(1)
     slots = cache.shape[2]
     lane = lax.broadcasted_iota(jnp.int32, (heads, slots), 1)
     mine = lax.bitwise_and(lane, heads - 1) == lax.broadcasted_iota(jnp.int32, (heads, slots), 0)
 
     @pl.loop(0, batch)
     def _(b):
+        @pl.when(b == 4)
+        def _():
+            reduce.middle(1)
+
         cache_load(b, 0).wait()
         cache_load(b, 1).wait()
         q, k_tok, v_tok = q_scr[b], kt_ref[b].astype(F32), vt_ref[b].astype(F32)
-        scores = dot_nt(q, cache[0, b]) * scale
+        row = lax.rem(b, ROW_SLOTS)
+        scores = dot_nt(q, cache[0, row]) * scale
         scores = jnp.where(mine & (lane < c_len[b] * heads), scores, MASKED)
         own = jnp.sum(q.astype(F32) * k_tok, axis=-1, keepdims=True) * scale
         top = jnp.maximum(jnp.max(scores, axis=-1, keepdims=True), own)
@@ -355,25 +423,150 @@
         total = jnp.sum(weights, axis=-1, keepdims=True) + own_w
         prob = (weights / total).astype(BF16)
         own_prob = (own_w / total).astype(BF16).astype(F32)
-        ctxd[b] = (dot(prob, cache[1, b]) + own_prob * v_tok).astype(BF16).astype(F32)
+        ctxd[b] = (dot(prob, cache[1, row]) + own_prob * v_tok).astype(BF16).astype(F32)
+
+        @pl.when(b + ROW_SLOTS < batch)
+        def _():
+            cache_load(b + ROW_SLOTS, 0).start()
+            cache_load(b + ROW_SLOTS, 1).start()
 
     by_head = jnp.swapaxes(ctxd[...], 0, 1)
     lhs_d = jnp.concatenate([by_head[h] for h in range(heads)], axis=1).astype(BF16)
     wo_load(1).wait()
     quarter = width // 4
     for c in range(4):
-        part_scr[c] = dot(lhs_d, wo_buf[1, :, c * quarter:(c + 1) * quarter])
+        part_scr[c] = wo_product(lhs_d, 1, slice(c * quarter, (c + 1) * quarter))
     for r in range(4):
         small.part[r] = part_scr[lax.bitwise_xor(y, r)]
     small.start()
+    f_start(2)
+    f_start(3)
+    for i in range(LATE_SLOTS):
+        late_load(i).start()
 
     piece = block // 2
-    for at, total in zip((0, 1), reduce.totals()):
+    parts = [reduce.totals(c) for c in range(GROUPS)]
+    for at in range(2):
+        total = jnp.concatenate([part[at] for part in parts], axis=1)
         x_rows = x_ref[pl.ds(pl.multiple_of(y * block + at * piece, piece), piece), :]
         h = (x_rows.astype(F32) + total.astype(BF16).astype(F32)).astype(BF16)
-        h_ref[at * piece:(at + 1) * piece, :] = h
+        own_ref[at * piece:(at + 1) * piece, :] = h
         rows_all[0, at] = rms(h.astype(F32), g_ref[1:2, :])
-    gather.start()
+    for c in range(GROUPS):
+        gather.start(c)
+    small.middle()
+    for c in range(GROUPS):
+        gather.forward(c)
+    small.finish(nd_ref)
+    h_dec = (tok_ref[...].astype(F32) + nd_ref[...].astype(F32)).astype(BF16)
+    hd_ref[...] = h_dec.astype(F32)
+    nd_ref[...] = rms(hd_ref[...], dg_ref[1:2, :])
+    part_scr[...] = jnp.zeros_like(part_scr)
+    reduce.drain()
+    for ref in (reduce.send_a, reduce.keep_a, reduce.send_b, reduce.keep_b):
+        ref[...] = jnp.zeros_like(ref)
+    gather.finish()
+    for copy in kv_copies:
+        copy.start()
+    for r in range(4):
+        for half in range(2):
+            i = (2 * r + half) * piece
+            n_ref[i:i + piece, :] = rows_all[r, half]
+
+    def gate_up(i, slot, n):
+        tall = n.shape[0] >= 128
+        gate, up = [(dot_nt(w, n) if tall else dot_nt(n, w)).astype(BF16).astype(F32) for w in (ring[3 * slot], ring[3 * slot + 1])]
+        m = jax.nn.silu(gate) * up
+        m = m.T if tall else m
+        lane = lax.broadcasted_iota(jnp.int32, m.shape, 1)
+        return jnp.where(f_at(i) + lane >= i * F_BLOCK, m, 0.0).astype(BF16)
+
+    def down(m, slot, size, add):
+        for c in range(size // N_BLOCK):
+            cols = slice(c * N_BLOCK, (c + 1) * N_BLOCK)
+            add(dot(m, ring[3 * slot + 2, :, cols]), cols)
+
+    def stream_mlp(base, gu_hbm, down_hbm, size, n_rows, m_ref, add, beside):
+        for copy in gu_loads(base, gu_hbm, 0):
+            copy.wait()
+        m_ref[0] = gate_up(0, f_slot(base), n_rows[...])
+
+        @pl.loop(1, f_steps)
+        def _(i):
+            t = base + i
+            f_start(t + F_SLOTS - 1)
+            slot = f_slot(t)
+            for copy in gu_loads(t, gu_hbm, i):
+                copy.wait()
+            down_load(t, down_hbm, i - 1, size).wait()
+            before = m_ref[i - 1]
+            after = gate_up(i, slot, n_rows[...])
+            down(before, slot, size, add)
+            m_ref[i] = after
+            beside(i)
+
+        t = base + f_steps
+        f_start(t + F_SLOTS - 1)
+        down_load(t, down_hbm, f_steps - 1, size).wait()
+        down(m_ref[f_steps - 1], f_slot(t), size, add)
+
+    def add_pre(part, cols):
+        reduce.put(part, cols, True)
+
+    stream_mlp(0, gup_hbm, dnp_hbm, group, n_ref, m_ref, add_pre, lambda i: None)
+    reduce.start(0)
+
+    @pl.loop(0, f_steps)
+    def _(i):
+        late_load(i).wait()
+        m = m_ref[i]
+        for c in range(group // N_BLOCK):
+            at = c * N_BLOCK
+            add_pre(dot(m, late[lax.rem(i, LATE_SLOTS), :, at:at + N_BLOCK]), slice(group + at, group + at + N_BLOCK))
+
+        @pl.when(i + LATE_SLOTS < f_steps)
+        def _():
+            late_load(i + LATE_SLOTS).start()
+
+    reduce.start(1)
+
+    def add_dec(part, cols):
+        c = cols.start // quarter
+        part_scr[c, :, cols.start - c * quarter:cols.stop - c * quarter] += part
+
+    def own_rows(c):
+        cols = slice(c * group, (c + 1) * group)
+        for half, total in zip((0, 1), reduce.totals(c)):
+            h = own_ref[half * piece:(half + 1) * piece, cols].astype(F32)
+            rows_all[0, half, :, cols] = (h + total.astype(BF16).astype(F32)).astype(BF16)
+        gather.start(c)
+
+    def between(i):
+        @pl.when(i == 1)
+        def _():
+            reduce.middle(0)
+
+        @pl.when(i == 5)
+        def _():
+            reduce.middle(1)
+
+        @pl.when(i == 6)
+        def _():
+            own_rows(0)
+
+        @pl.when(i == 8)
+        def _():
+            gather.forward(0)
+
+        @pl.when(i == 9)
+        def _():
+            own_rows(1)
+
+    stream_mlp(f_steps, gud_hbm, dnd_hbm, width, nd_ref, md_ref, add_dec, between)
+    for r in range(4):
+        small.part[r] = part_scr[lax.bitwise_xor(y, r)]
+    small.start()
+    gather.forward(1)
     small.middle()
     for r in range(4):
         kv_copies[r].wait_recv()
@@ -383,129 +576,11 @@
             v_scr[owner * (heads // 4) + jj] = kv_got[r, 1, jj]
     kp_ref[...] = jnp.swapaxes(k_scr[...], 0, 1)
     vp_ref[...] = jnp.swapaxes(v_scr[...], 0, 1)
-    gather.forward()
-    small.finish(a_ref)
+    small.finish(nd_ref)
+    d_out[...] = (hd_ref[...] + nd_ref[...].astype(F32)).astype(BF16)
     reduce.drain()
     for copy in kv_copies:
         copy.wait_send()
-    gather.finish()
-    n_out[...] = rows_all[...]
-
-
-def mlp_kernel(n_all, own_ref, tok_ref, a_ref, dg_ref, gup_hbm, dnp_hbm, gud_hbm, dnd_hbm, h_out, d_out,
-               g_buf, u_buf, d_buf, sem, n_ref, nd_ref, hd_ref, part_scr, *comm):
-    y = lax.axis_index('tp')
-    peers = [{'tp': lax.bitwise_xor(y, r)} for r in (1, 2, 3)]
-    reduce = RowReduce(y, comm[:12])
-    rows_all = comm[12]
-    gather = RowGather(y, *comm[12:15])
-    small = ColumnSum(y, comm[15:20])
-    ff, width = dnp_hbm.shape
-    steps = pl.cdiv(ff, F_BLOCK)
-    quarter = width // 4
-
-    def at(i):
-        return pl.multiple_of(jnp.minimum(i * F_BLOCK, ff - F_BLOCK), 8)
-
-    def loads(i, gu_hbm, down_hbm, slot):
-        rows = pl.ds(at(i), F_BLOCK)
-        return (pltpu.make_async_copy(gu_hbm.at[0, rows], g_buf.at[slot], sem.at[0, slot]),
-                pltpu.make_async_copy(gu_hbm.at[1, rows], u_buf.at[slot], sem.at[1, slot]),
-                pltpu.make_async_copy(down_hbm.at[rows], d_buf.at[slot], sem.at[2, slot]))
-
-    def product(i, slot, n, add):
-        gate = dot_nt(n, g_buf[slot]).astype(BF16).astype(F32)
-        up = dot_nt(n, u_buf[slot]).astype(BF16).astype(F32)
-        m = jax.nn.silu(gate) * up
-        lane = lax.broadcasted_iota(jnp.int32, m.shape, 1)
-        m = jnp.where(at(i) + lane >= i * F_BLOCK, m, 0.0).astype(BF16)
-        for c in range(width // N_BLOCK):
-            cols = slice(c * N_BLOCK, (c + 1) * N_BLOCK)
-            add(dot(m, d_buf[slot, :, cols]), cols)
-
-    for i in range(F_SLOTS - 1):
-        for copy in loads(i, gup_hbm, dnp_hbm, i):
-            copy.start()
-    greet(peers)
-    rows = n_ref.shape[0]
-    piece = rows // 8
-    for r in range(4):
-        for half in range(2):
-            i = (2 * r + half) * piece
-            n_ref[i:i + piece, :] = n_all[r, half]
-    for ref in (reduce.send_a, reduce.keep_a, reduce.send_b, reduce.keep_b, part_scr):
-        ref[...] = jnp.zeros_like(ref)
-    h_dec = (tok_ref[...].astype(F32) + a_ref[...].astype(F32)).astype(BF16)
-    hd_ref[...] = h_dec.astype(F32)
-    nd_ref[...] = rms(hd_ref[...], dg_ref[1:2, :])
-
-    @pl.loop(0, steps)
-    def _(i):
-        j = i + F_SLOTS - 1
-
-        @pl.when(j < steps)
-        def _():
-            for copy in loads(j, gup_hbm, dnp_hbm, lax.rem(j, F_SLOTS)):
-                copy.start()
-
-        @pl.when(j >= steps)
-        def _():
-            for copy in loads(j - steps, gud_hbm, dnd_hbm, lax.rem(j, F_SLOTS)):
-                copy.start()
-
-        slot = lax.rem(i, F_SLOTS)
-        for copy in loads(i, gup_hbm, dnp_hbm, slot):
-            copy.wait()
-        product(i, slot, n_ref[...], lambda part, cols: reduce.put(part, cols, True))
-
-    greeted(peers)
-    for c in range(GROUPS):
-        reduce.start(c)
-
-    def add_dec(part, cols):
-        c = cols.start // quarter
-        part_scr[c, :, cols.start - c * quarter:cols.stop - c * quarter] += part
-
-    def own_rows():
-        for half, total in zip((0, 1), reduce.totals()):
-            h = own_ref[half * piece:(half + 1) * piece, :].astype(F32)
-            rows_all[0, half] = (h + total.astype(BF16).astype(F32)).astype(BF16)
-        gather.start()
-
-    @pl.loop(0, steps)
-    def _(i):
-        j = i + F_SLOTS - 1
-
-        @pl.when(j < steps)
-        def _():
-            for copy in loads(j, gud_hbm, dnd_hbm, lax.rem(j + steps, F_SLOTS)):
-                copy.start()
-
-        slot = lax.rem(i + steps, F_SLOTS)
-        for copy in loads(i, gud_hbm, dnd_hbm, slot):
-            copy.wait()
-        product(i, slot, nd_ref[...], add_dec)
-
-        @pl.when(i == 2)
-        def _():
-            reduce.middle(0)
-
-        @pl.when(i == 5)
-        def _():
-            reduce.middle(1)
-
-        @pl.when(i == 8)
-        def _():
-            own_rows()
-
-    for r in range(4):
-        small.part[r] = part_scr[lax.bitwise_xor(y, r)]
-    small.start()
-    gather.forward()
-    small.middle()
-    small.finish(nd_ref)
-    d_out[...] = (hd_ref[...] + nd_ref[...].astype(F32)).astype(BF16)
-    reduce.drain()
     gather.finish()
     for r in range(4):
         owner = lax.bitwise_xor(y, r)
@@ -513,8 +588,9 @@
             h_out[pl.ds(pl.multiple_of((2 * owner + half) * piece, piece), piece), :] = rows_all[r, half]
 
 
-def cache_kernel(c_len, kt_ref, vt_ref, kc_hbm, vc_hbm, kn_hbm, vn_hbm, cache, in_sem, out_sem):
+def finish_kernel(c_len, kt_ref, vt_ref, kc_hbm, vc_hbm, h_in, d_in, kp_in, vp_in, kn_hbm, vn_hbm, h_hbm, d_hbm, kp_hbm, vp_hbm, cache, h_buf, d_buf, kp_buf, vp_buf, in_sem, out_sem, m_in, m_out):
     batch = kt_ref.shape[0]
+    moved = ((h_in, h_buf, h_hbm), (d_in, d_buf, d_hbm), (kp_in, kp_buf, kp_hbm), (vp_in, vp_buf, vp_hbm))
 
     def load(b, which):
         return pltpu.make_async_copy((kc_hbm, vc_hbm)[which].at[b], cache.at[which, b], in_sem.at[which, b])
@@ -526,6 +602,11 @@
     def _(b):
         load(b, 0).start()
         load(b, 1).start()
+
+    ins = [pltpu.make_async_copy(src, mid, m_in.at[i]) for i, (src, mid, _) in enumerate(moved)]
+    outs = [pltpu.make_async_copy(mid, dst, m_out.at[i]) for i, (_, mid, dst) in enumerate(moved)]
+    for copy in ins:
+        copy.start()
 
     @pl.loop(0, batch)
     def _(b):
@@ -534,10 +615,17 @@
             cache[which, b, c_len[b]] = tok[b]
             store(b, which).start()
 
+    for first, second in zip(ins, outs):
+        first.wait()
+        second.start()
+
     @pl.loop(0, batch)
     def _(b):
         store(b, 0).wait()
         store(b, 1).wait()
+
+    for copy in outs:
+        copy.wait()
 
 
 def call(kernel, name, in_specs, out_specs, out_shape, scratch, us, collective_id=None):
@@ -568,31 +656,32 @@
         piece = rows // 8
         quarter = width // 4
         pairs = heads // 2
+        f_steps = pl.cdiv(w_down_pre.shape[1], F_BLOCK)
         dma = pltpu.SemaphoreType.DMA
         cos_tab, sin_tab = rope_rows(max(rows, cache_len), head)
         comm = RowReduce.scratch(piece, width) + RowGather.scratch(piece, width) + ColumnSum.scratch(batch, quarter)
         flat = (batch, cache_len * heads, head)
         wide = (batch, cache_len, heads, head)
         kv_block = pltpu.VMEM((4, 2, heads // 4, rows, head), BF16)
-        h_own, n_all, a_all, k_tok, v_tok, k_prompt, v_prompt = call(
-            functools.partial(attn_kernel, side), 'attn', [SMEM] * 2 + [VMEM] * 6 + [HBM] * 6, [VMEM] * 7,
-            [shape((2 * piece, width), BF16), shape((4, 2, piece, width), BF16), shape((batch, width), BF16)] + [shape((batch, heads, head), BF16)] * 2 + [shape((rows, heads, head), BF16)] * 2,
-            [pltpu.VMEM((D_SLOTS, D_BLOCK, 3, heads, head), BF16), dma((D_SLOTS,)), pltpu.VMEM((2, heads * head, width), BF16), dma((2,)),
-             pltpu.VMEM((2,) + flat, BF16), dma((2, batch)),
+        rows_shape, tok_shape, kv_shape, out_shape = shape((rows, width), BF16), shape((batch, heads, head), BF16), shape((rows, heads, head), BF16), shape((batch, width), BF16)
+        h_out, dec_out, k_tok, v_tok, k_prompt, v_prompt = call(
+            functools.partial(layer_kernel, side), 'layer', [SMEM] * 2 + [VMEM] * 5 + [HBM] * 11, [VMEM] * 6,
+            [rows_shape, out_shape, tok_shape, tok_shape, kv_shape, kv_shape],
+            [pltpu.VMEM((rows, width), BF16), dma, pltpu.VMEM((D_SLOTS, D_BLOCK, 3, heads, head), BF16), dma((D_SLOTS,)),
+             pltpu.VMEM((3 * F_SLOTS, F_BLOCK, width), BF16), dma((3, F_SLOTS)), dma((2,)), pltpu.VMEM((2, ROW_SLOTS) + flat[1:], BF16), dma((2, ROW_SLOTS)),
              pltpu.VMEM((rows, width), BF16), pltpu.VMEM((3 * pairs, rows, 2 * head), F32), pltpu.VMEM((rows, heads * head), BF16), pltpu.VMEM((rows, heads * head), BF16),
              pltpu.VMEM((heads, rows, head), BF16), pltpu.VMEM((heads, rows, head), BF16),
-             pltpu.VMEM((batch, width), BF16), pltpu.VMEM((3 * pairs, batch, 2 * head), F32), pltpu.VMEM((batch, heads, head), BF16), pltpu.VMEM((batch, heads, head), F32), pltpu.VMEM((4, batch, quarter), F32),
-             kv_block, kv_block, dma((4,)), dma((4,))] + comm, 46, 0)(
-            s_len, c_len, prompt_x, gain_pre[0], cos_tab, sin_tab, dec_tokens, gain_dec[0],
-            w_qkv_pre[0], w_out_pre.reshape(heads * head, width), w_qkv_dec.reshape(width, 3, heads, head),
-            k_cache.reshape(flat), v_cache.reshape(flat), w_out_dec.reshape(heads * head, width))
-        h_out, dec_out = call(
-            mlp_kernel, 'mlp', [VMEM] * 5 + [HBM] * 4, [VMEM] * 2, [shape((rows, width), BF16), shape((batch, width), BF16)],
-            [pltpu.VMEM((F_SLOTS, F_BLOCK, width), BF16)] * 3 + [dma((3, F_SLOTS)), pltpu.VMEM((rows, width), BF16), pltpu.VMEM((batch, width), BF16), pltpu.VMEM((batch, width), F32), pltpu.VMEM((4, batch, quarter), F32)] + comm, 50, 1)(
-            n_all, h_own, dec_tokens, a_all, gain_dec[0], w_gu_pre[0], w_down_pre[0], w_gu_dec[0], w_down_dec[0])
-        k_new, v_new = call(
-            cache_kernel, 'cache', [SMEM] + [VMEM] * 2 + [HBM] * 2, [HBM] * 2, [shape(wide, BF16)] * 2,
-            [pltpu.VMEM((2,) + wide, BF16), dma((2, batch)), dma((2, batch))], 7)(c_len, k_tok, v_tok, k_cache.reshape(wide), v_cache.reshape(wide))
+             pltpu.VMEM((batch, width), BF16), pltpu.VMEM((batch, width), F32), pltpu.VMEM((3 * pairs, batch, 2 * head), F32), pltpu.VMEM((batch, heads, head), BF16), pltpu.VMEM((batch, heads, head), F32), pltpu.VMEM((4, batch, quarter), F32),
+              pltpu.VMEM((2 * piece, width), BF16), pltpu.VMEM((f_steps, rows, F_BLOCK), BF16), pltpu.VMEM((f_steps, batch, F_BLOCK), BF16), pltpu.VMEM((LATE_SLOTS, F_BLOCK, width // GROUPS), BF16), dma((LATE_SLOTS,)), kv_block, kv_block, dma((4,)), dma((4,))] + comm, 90, 0)(
+            s_len, c_len, gain_pre[0], cos_tab, sin_tab, dec_tokens, gain_dec[0], prompt_x,
+            w_qkv_pre[0], w_out_pre.reshape(heads * head // F_BLOCK, F_BLOCK, width), w_qkv_dec.reshape(width, 3, heads, head),
+            k_cache.reshape(flat), v_cache.reshape(flat), w_out_dec.reshape(heads * head // F_BLOCK, F_BLOCK, width),
+            w_gu_pre[0], w_down_pre[0], w_gu_dec[0], w_down_dec[0])
+        k_new, v_new, h_out, dec_out, k_prompt, v_prompt = call(
+            finish_kernel, 'finish', [SMEM] + [VMEM] * 2 + [HBM] * 6, [HBM] * 6, [shape(wide, BF16)] * 2 + [rows_shape, out_shape, kv_shape, kv_shape],
+            [pltpu.VMEM((2,) + wide, BF16), pltpu.VMEM((rows, width), BF16), pltpu.VMEM((batch, width), BF16), pltpu.VMEM((rows, heads, head), BF16), pltpu.VMEM((rows, heads, head), BF16),
+             dma((2, batch)), dma((2, batch)), dma((4,)), dma((4,))], 7)(
+            c_len, k_tok, v_tok, k_cache.reshape(wide), v_cache.reshape(wide), h_out, dec_out, k_prompt, v_prompt)
         prompt_shape = (1, rows, heads, 1, head)
         return h_out, dec_out, k_prompt.reshape(prompt_shape), v_prompt.reshape(prompt_shape), k_new.reshape(k_cache.shape), v_new.reshape(v_cache.shape)
 

time: 134 us -> 118 us (0.88)
  Pallas kernels: 127 us -> 117 us
  local copies, waits for them, and re-layouts: 5.17 us -> 0 us
    pallas_call x3 -> x2, Pallas kernels: 127 us -> 117 us  [the longest x1 108 us: device_fn(): call(functools.partial(layer_kernel, side), 'layer', [SMEM] * 2 + [VMEM]...]
    unnamed x8 -> x0, local copies, waits for them, and re-layouts: 5.17 us -> none
where the time goes in v2:
time: 118 us
  Pallas kernels  117 us (99%)
  between operations  1.29 us (1%)
    pallas_call x1, Pallas kernels, device_fn(): call(functools.partial(layer_kernel, side), 'layer', [SMEM] * 2 + [VMEM]...  108 us
    pallas_call x1, Pallas kernels, device_fn(): call(finish_kernel, 'finish', [SMEM] + [VMEM] * 2 + [HBM] * 6, [HBM] * 6,...  8.72 us

profile of v2, /device:TPU:100, one launch (start us, length us, event | category | flops | bytes accessed | tf_op | source)
XLA Modules:
  0.0 118.2 jit_solution(14100729369581122778)
XLA Ops:
  1.3 108.2 %layer.1 = (bf16[128,4096]{1,0:T(8,128)(2,1)}, bf16[8,4096]{1,0:T(8,128)(2,1)}, bf16[8,8,128]{2,1,0:T(8,128)(2,1)}, bf16[8,8,128]{2,1,0:T(8,128)(2,1)}, bf16[128...) custom-call(s32[1]{0:T(128)S(6)} %copy.28.s_len, s32[8]{0:T(128)} %c_len.3, f32[2,4096]{1,0:T(2,128)} %bitcast.38, ...), custom_call_target="tpu_custom_call" | custom-call | flops 1800000000 | bytes 270000000 | tf_op jit(solution)/shard_map/layer/pallas_call | solution.py:667
  109.5 8.7 %finish.1 = (bf16[8,256,8,128]{3,2,1,0:T(8,128)(2,1)}, bf16[8,256,8,128]{3,2,1,0:T(8,128)(2,1)}, bf16[128,4096]{1,0:T(8,128)(2,1)}, bf16[8,4096]{1,0:T(8,128)(2,...) custom-call(s32[8]{0:T(128)} %c_len.3, bf16[8,8,128]{2,1,0:T(8,128)(2,1)} %get-tuple-element.18.kt_ref, ...), custom_call_target="tpu_custom_call" | custom-call | flops 140000000 | bytes 21000000 | tf_op jit(solution)/shard_map/finish/pallas_call | solution.py:680

commit v3 on v2

--- a/solution.py
+++ b/solution.py
@@ -203,9 +203,9 @@
                 copy.wait_send()
 
 
-def layer_kernel(side, s_len, c_len, g_ref, cos_ref, sin_ref, tok_ref, dg_ref, x_hbm, wp_hbm, wop_hbm, wd_hbm, kc_hbm, vc_hbm, wod_hbm, gup_hbm, dnp_hbm, gud_hbm, dnd_hbm,
+def layer_kernel(side, s_len, c_len, g_hbm, cos_hbm, sin_hbm, tok_hbm, dg_hbm, x_hbm, wp_hbm, wop_hbm, wd_hbm, kc_hbm, vc_hbm, wod_hbm, gup_hbm, dnp_hbm, gud_hbm, dnd_hbm,
                  h_out, d_out, kt_ref, vt_ref, kp_ref, vp_ref,
-                 x_ref, x_sem, buf, sem, ring, ring_sem, wo_sem, cache, cache_sem, n_ref, acc, ctx, ctx_rel, k_scr, v_scr, nd_ref, hd_ref, accd, q_scr, ctxd, part_scr, own_ref, m_ref, md_ref, late, late_sem,
+                 x_ref, g_ref, cos_ref, sin_ref, tok_ref, dg_ref, x_sem, buf, sem, ring, ring_sem, wo_sem, cache, cache_sem, n_ref, acc, ctx, ctx_rel, k_scr, v_scr, nd_ref, hd_ref, accd, q_scr, ctxd, part_scr, own_ref, m_ref, md_ref, late, late_sem,
                  kv_send, kv_got, kv_ssem, kv_rsem, *comm):
     y = lax.axis_index('tp')
     s = lax.axis_index('side')
@@ -274,13 +274,15 @@
         slot = lax.rem(i, LATE_SLOTS)
         return pltpu.make_async_copy(dnp_hbm.at[pl.ds(f_at(i), F_BLOCK), pl.ds(group, group)], late.at[slot], late_sem.at[slot])
 
-    x_copy = pltpu.make_async_copy(x_hbm, x_ref, x_sem)
-    x_copy.start()
+    smalls = [pltpu.make_async_copy(src, dst, x_sem.at[i]) for i, (src, dst) in enumerate(((x_hbm, x_ref), (g_hbm, g_ref), (cos_hbm, cos_ref), (sin_hbm, sin_ref), (tok_hbm, tok_ref), (dg_hbm, dg_ref)))]
+    for copy in smalls:
+        copy.start()
     load(0, wp_hbm, 0).start()
     greet(near_peers + far_peers)
     acc[...] = jnp.zeros_like(acc)
     accd[...] = jnp.zeros_like(accd)
-    x_copy.wait()
+    for copy in smalls:
+        copy.wait()
     for i in range(1, D_SLOTS - 1):
         load(i, wp_hbm, i).start()
 
@@ -665,9 +667,9 @@
         kv_block = pltpu.VMEM((4, 2, heads // 4, rows, head), BF16)
         rows_shape, tok_shape, kv_shape, out_shape = shape((rows, width), BF16), shape((batch, heads, head), BF16), shape((rows, heads, head), BF16), shape((batch, width), BF16)
         h_out, dec_out, k_tok, v_tok, k_prompt, v_prompt = call(
-            functools.partial(layer_kernel, side), 'layer', [SMEM] * 2 + [VMEM] * 5 + [HBM] * 11, [VMEM] * 6,
+            functools.partial(layer_kernel, side), 'layer', [SMEM] * 2 + [HBM] * 16, [VMEM] * 6,
             [rows_shape, out_shape, tok_shape, tok_shape, kv_shape, kv_shape],
-            [pltpu.VMEM((rows, width), BF16), dma, pltpu.VMEM((D_SLOTS, D_BLOCK, 3, heads, head), BF16), dma((D_SLOTS,)),
+            [pltpu.VMEM((rows, width), BF16), pltpu.VMEM((2, width), F32), pltpu.VMEM(cos_tab.shape, F32), pltpu.VMEM(cos_tab.shape, F32), pltpu.VMEM((batch, width), BF16), pltpu.VMEM((2, width), F32), dma((6,)), pltpu.VMEM((D_SLOTS, D_BLOCK, 3, heads, head), BF16), dma((D_SLOTS,)),
              pltpu.VMEM((3 * F_SLOTS, F_BLOCK, width), BF16), dma((3, F_SLOTS)), dma((2,)), pltpu.VMEM((2, ROW_SLOTS) + flat[1:], BF16), dma((2, ROW_SLOTS)),
              pltpu.VMEM((rows, width), BF16), pltpu.VMEM((3 * pairs, rows, 2 * head), F32), pltpu.VMEM((rows, heads * head), BF16), pltpu.VMEM((rows, heads * head), BF16),
              pltpu.VMEM((heads, rows, head), BF16), pltpu.VMEM((heads, rows, head), BF16),

time: 118 us -> 117 us (level)
    pallas_call x1, Pallas kernels: 108 us -> 107 us  [device_fn(): call(functools.partial(layer_kernel, side), 'layer', [SMEM] * 2 + [HBM] *...]
where the time goes in v3:
time: 117 us
  Pallas kernels  116 us (99%)
  between operations  1.29 us (1%)
    pallas_call x1, Pallas kernels, device_fn(): call(functools.partial(layer_kernel, side), 'layer', [SMEM] * 2 + [HBM] *...  107 us
    pallas_call x1, Pallas kernels, device_fn(): call(finish_kernel, 'finish', [SMEM] + [VMEM] * 2 + [HBM] * 6, [HBM] * 6,...  8.72 us

profile of v3, /device:TPU:100, one launch (start us, length us, event | category | flops | bytes accessed | tf_op | source)
XLA Modules:
  0.0 117.0 jit_solution(10421010372897725537)
XLA Ops:
  1.3 107.0 %layer.1 = (bf16[128,4096]{1,0:T(8,128)(2,1)}, bf16[8,4096]{1,0:T(8,128)(2,1)}, bf16[8,8,128]{2,1,0:T(8,128)(2,1)}, bf16[8,8,128]{2,1,0:T(8,128)(2,1)}, bf16[128...) custom-call(s32[1]{0:T(128)S(6)} %copy.28.s_len, s32[8]{0:T(128)} %c_len.3, f32[2,4096]{1,0:T(2,128)} %bitcast.38, ...), custom_call_target="tpu_custom_call" | custom-call | flops 1800000000 | bytes 270000000 | tf_op jit(solution)/shard_map/layer/pallas_call | solution.py:669
  108.3 8.7 %finish.1 = (bf16[8,256,8,128]{3,2,1,0:T(8,128)(2,1)}, bf16[8,256,8,128]{3,2,1,0:T(8,128)(2,1)}, bf16[128,4096]{1,0:T(8,128)(2,1)}, bf16[8,4096]{1,0:T(8,128)(2,...) custom-call(s32[8]{0:T(128)} %c_len.3, bf16[8,8,128]{2,1,0:T(8,128)(2,1)} %get-tuple-element.18.kt_ref, ...), custom_call_target="tpu_custom_call" | custom-call | flops 140000000 | bytes 21000000 | tf_op jit(solution)/shard_map/finish/pallas_call | solution.py:682
